TPU v7x, 32 devices: a whole 2x2x4 slice. The times are simulated.
32 devices in a mesh: section: 4 (over y, x), ctx: 8 (over z, core).
Axes of the slice: x: 2, y: 2, z: 4, core: 2. Of those that a mesh axis runs over, the one named last changes fastest.
Arguments:
- queries: bfloat16 [4, 8, 1024, 512], P('section', None, 'ctx'), may hold values from -5 to 5
- keys: bfloat16 [4, 8, 1024, 128], P('section', None, 'ctx'), may hold values from -5 to 5
- values: bfloat16 [4, 8, 1024, 128], P('section', None, 'ctx'), may hold values from -6 to 6
- out_grad: bfloat16 [4, 1024, 512], P('section', 'ctx'), may hold values from -6 to 6
- stretch_ids: int32 [16], P('ctx'), may hold values from 0 to 15, as said below
- stash_slot: int32 [4], P('section'), may hold values from 0 to 7
Outputs:
- passed_grads: bfloat16 [4, 1024, 768], P('section', 'ctx')
Inputs may be any that keep to these rules, and one draw needn't show every extreme that they name: `stretch_ids`: for each sequence, the entries of its 8 row blocks (two a block, blocks in order) are a permutation of 0 to 15 in which a block's two entries are some c and 15 - c, in either order.
All inputs are finite; a program needn't handle non-finite values.
Results may differ from a plain program's by a relative error of at most 0.035.
Values may be sent and summed in bfloat16 or wider, within the bound.
No kernel may reach another device: no remote copies, remote signals or barrier semaphores. Data moves between devices by JAX's collectives and lax.ppermute only.
A program may use at most 64 MiB of HBM per device.

v0:
```python
import functools
import math

import jax
import jax.numpy as jnp
from jax import lax
from jax.experimental import pallas as pl
from jax.experimental.pallas import tpu as pltpu
from jax.sharding import PartitionSpec as P


MASKED = -1e30
FLOOR = -1e29
ID_ROWS = 8
LOG2E = 1.4426950408889634
VMEM_GRANT = 8 * 1024 * 1024


def vmem_spec():
    return pl.BlockSpec(memory_space=pltpu.VMEM)


def in_hbm(value):
    return pltpu.with_memory_space_constraint(value, pltpu.HBM)


def hbm_spec():
    return pl.BlockSpec(memory_space=pltpu.HBM)


def partner_swap(value, count):
    return lax.ppermute(value, "ctx", [(i, i ^ 1) for i in range(count)])


def chip_pairs(count, step):
    chips = count // 2
    if chips & (chips - 1) == 0:
        target = [z ^ step for z in range(chips)]
    else:
        target = [(z + step) % chips for z in range(chips)]
    return [(2 * z + k, 2 * target[z] + k) for z in range(chips) for k in range(2)]


def chip_send(value, count, step):
    return lax.ppermute(value, "ctx", chip_pairs(count, step))


def chip_return(value, count, step):
    return lax.ppermute(value, "ctx", [(b, a) for a, b in chip_pairs(count, step)])


def fetch_kernel(slot_ref, ids_ref, query_ref, key_ref, value_ref, grad_ref, kv_ref, qg_ref, ids, sems):
    rows, head = key_ref.shape[2:]
    group = query_ref.shape[3] // head
    slot = slot_ref[0]
    ids_copy = pltpu.make_async_copy(ids_ref, ids, sems.at[0])
    copies = [
        pltpu.make_async_copy(key_ref.at[0, slot], kv_ref.at[0:rows, 0:head], sems.at[1]),
        pltpu.make_async_copy(value_ref.at[0, slot], kv_ref.at[0:rows, head : 2 * head], sems.at[2]),
    ]
    for h in range(group):
        cols = slice(h * head, (h + 1) * head)
        query_to = qg_ref.at[h * rows : (h + 1) * rows]
        grad_to = qg_ref.at[(group + h) * rows : (group + h + 1) * rows]
        copies.append(
            pltpu.make_async_copy(query_ref.at[0, slot, :, cols], query_to, sems.at[3 + 2 * h])
        )
        copies.append(pltpu.make_async_copy(grad_ref.at[0, :, cols], grad_to, sems.at[4 + 2 * h]))
    ids_copy.start()
    for copy in copies:
        copy.start()
    ids_copy.wait()
    half = ID_ROWS // 2
    row = lax.broadcasted_iota(jnp.int32, (ID_ROWS, 2 * head), 0)
    lines = jnp.where(row < half, ids[0], ids[1]).astype(jnp.float32).astype(jnp.bfloat16)
    kv_ref[rows : rows + ID_ROWS, :] = lines
    qg_ref[2 * group * rows : 2 * group * rows + ID_ROWS, :] = lines[:, 0:head]
    for copy in copies:
        copy.wait()


def id_lines(ref, start, width):
    half = ID_ROWS // 2
    lines = ref[start : start + ID_ROWS, 0:width].astype(jnp.float32)
    return lines[0:1], lines[half : half + 1]


def lane_positions(qg_ref, group, rows, head):
    stretch = rows // 2
    first, second = id_lines(qg_ref, 2 * group * rows, head)
    lane = lax.broadcasted_iota(jnp.int32, (1, rows), 1)
    base = jnp.where(lane < stretch, first, second) * stretch
    offset = jnp.where(lane < stretch, lane, lane - stretch).astype(jnp.float32)
    one_head = base + offset
    return jnp.concatenate([one_head] * group, axis=1)


def dot_nt(a, b):
    return lax.dot_general(a, b, (((1,), (1,)), ((), ())), preferred_element_type=jnp.float32)


def dot_nn(a, b):
    return lax.dot_general(a, b, (((1,), (0,)), ((), ())), preferred_element_type=jnp.float32)


def dot_tn(a, b):
    return lax.dot_general(a, b, (((0,), (0,)), ((), ())), preferred_element_type=jnp.float32)


def score_kernel(group, rows, head, earlier, *refs):
    qg_refs, kv_ref = refs[0:2], refs[2]
    earlier_refs = refs[3 : 3 + earlier]
    exp_ref, dprob_ref, stat_ref = refs[3 + earlier : 6 + earlier]
    width = group * rows
    stretch = rows // 2
    scale = LOG2E / math.sqrt(head)
    in_stretch = lax.broadcasted_iota(jnp.int32, (stretch, 1), 0).astype(jnp.float32)
    ids = id_lines(kv_ref, rows, head)
    key, value = kv_ref[0:rows, 0:head], kv_ref[0:rows, head : 2 * head]
    for b in range(2):
        lanes = slice(b * width, (b + 1) * width)
        place = lane_positions(qg_refs[b], group, rows, head)
        query = qg_refs[b][0:width, :]
        grad = qg_refs[b][width : 2 * width, :]
        scores = dot_nt(key, query) * scale
        dprob = dot_nt(value, grad)
        pieces = []
        for part in range(2):
            limit = place - stretch * jnp.concatenate([ids[part]] * group, axis=1)
            piece = scores[part * stretch : (part + 1) * stretch]
            pieces.append(jnp.where(in_stretch <= limit, piece, MASKED))
        scores = jnp.concatenate(pieces, axis=0)
        top = jnp.maximum(jnp.max(scores, axis=0, keepdims=True), FLOOR)
        raised = jnp.exp2(scores - top)
        exp_ref[:, lanes] = raised
        dprob_ref[:, lanes] = dprob
        stat_ref[0:1, lanes] = top
        stat_ref[1:2, lanes] = jnp.sum(raised, axis=0, keepdims=True)
        stat_ref[2:3, lanes] = jnp.sum(raised * dprob, axis=0, keepdims=True)
        stat_ref[3:8, lanes] = jnp.zeros((5, width), jnp.float32)
    if earlier:
        merged_ref = refs[6 + earlier]
        parts = [ref[...] for ref in earlier_refs] + [stat_ref[...]]
        top = functools.reduce(jnp.maximum, [part[0:1] for part in parts])
        fades = [jnp.exp2(part[0:1] - top) for part in parts]
        merged_ref[0:1, :] = top
        merged_ref[1:2, :] = sum(part[1:2] * fade for part, fade in zip(parts, fades))
        merged_ref[2:3, :] = sum(part[2:3] * fade for part, fade in zip(parts, fades))
        merged_ref[3:8, :] = jnp.zeros((5, 2 * width), jnp.float32)


def block_grads(group, rows, head, refs, dkv_ref, dscore_ref):
    exp_ref, dprob_ref, stat_ref, merged_ref, other_ref = refs[0:5]
    qg_refs = refs[5:7]
    width = group * rows
    dk = dv = None
    for b in range(2):
        lanes = slice(b * width, (b + 1) * width)
        swapped = slice((1 - b) * width, (2 - b) * width)
        top, total, mixed = (merged_ref[i : i + 1, lanes] for i in range(3))
        top_o, total_o, mixed_o = (other_ref[i : i + 1, swapped] for i in range(3))
        high = jnp.maximum(top, top_o)
        own, other = jnp.exp2(top - high), jnp.exp2(top_o - high)
        inverse = 1.0 / (total * own + total_o * other)
        delta = (mixed * own + mixed_o * other) * inverse
        fade = jnp.exp2(stat_ref[0:1, lanes] - high) * inverse
        probs = exp_ref[:, lanes] * fade
        dscore = (probs * (dprob_ref[:, lanes] - delta)).astype(jnp.bfloat16)
        dscore_ref[:, lanes] = dscore
        dk_part = dot_nn(dscore, qg_refs[b][0:width, :])
        dv_part = dot_nn(probs.astype(jnp.bfloat16), qg_refs[b][width : 2 * width, :])
        dk = dk_part if dk is None else dk + dk_part
        dv = dv_part if dv is None else dv + dv_part
    dkv_ref[:, 0:head] = (dk * (1.0 / math.sqrt(head))).astype(dkv_ref.dtype)
    dkv_ref[:, head : 2 * head] = dv.astype(dkv_ref.dtype)


def far_grad_kernel(group, rows, head, *refs):
    block_grads(group, rows, head, refs[0:7], refs[7], refs[8])


def near_grad_kernel(blocks, group, rows, head, *refs):
    kv_refs = refs[7 : 7 + blocks]
    dscore_refs = refs[7 + blocks : 6 + 2 * blocks]
    dkv_ref, dq_own_ref, dq_other_ref, dscore_ref = refs[6 + 2 * blocks :]
    width = group * rows
    scale = 1.0 / math.sqrt(head)
    block_grads(group, rows, head, refs[0:7], dkv_ref, dscore_ref)
    for b, dq_ref in enumerate((dq_own_ref, dq_other_ref)):
        lanes = slice(b * width, (b + 1) * width)
        dq = None
        for kv_ref, ref in zip(kv_refs, (dscore_ref,) + tuple(dscore_refs)):
            part = dot_tn(kv_ref[0:rows, 0:head], ref[:, lanes])
            dq = part if dq is None else dq + part
        for h in range(group):
            piece = jnp.transpose(dq[:, h * rows : (h + 1) * rows]) * scale
            dq_ref[:, h * head : (h + 1) * head] = piece.astype(dq_ref.dtype)


def params():
    return pltpu.CompilerParams(vmem_limit_bytes=VMEM_GRANT)


def per_device(queries, keys, values, out_grad, stretch_ids, stash_slot):
    rows, head = keys.shape[2:]
    group = queries.shape[3] // head
    width = group * rows
    count = lax.axis_size("ctx")
    blocks = count // 2
    sections = lax.axis_size("section")

    kv, qg = pl.pallas_call(
        fetch_kernel,
        out_shape=(
            jax.ShapeDtypeStruct((rows + ID_ROWS, 2 * head), jnp.bfloat16),
            jax.ShapeDtypeStruct((2 * width + ID_ROWS, head), jnp.bfloat16),
        ),
        in_specs=[pl.BlockSpec(memory_space=pltpu.SMEM)] + [hbm_spec()] * 5,
        out_specs=(vmem_spec(), vmem_spec()),
        scratch_shapes=[
            pltpu.SMEM(stretch_ids.shape, jnp.int32),
            pltpu.SemaphoreType.DMA((3 + 2 * group,)),
        ],
        compiler_params=params(),
        name="fetch",
    )(stash_slot, *(in_hbm(x) for x in (stretch_ids, queries, keys, values, out_grad)))

    steps = send_order(count)
    arrivals = arrival_order(count)
    kv_blocks = {0: kv}
    for j in steps:
        kv_blocks[j] = chip_send(kv, count, j)
    qg_other = partner_swap(qg, count)

    square = jax.ShapeDtypeStruct((rows, 2 * width), jnp.float32)
    lines = jax.ShapeDtypeStruct((8, 2 * width), jnp.float32)
    scored = {}
    for j in [0] + arrivals:
        last = j == arrivals[-1]
        earlier = [scored[i][2] for i in scored] if last else []
        scored[j] = pl.pallas_call(
            functools.partial(score_kernel, group, rows, head, len(earlier)),
            out_shape=(square, square, lines) + ((lines,) if last else ()),
            in_specs=[vmem_spec()] * (3 + len(earlier)),
            out_specs=(vmem_spec(),) * (4 if last else 3),
            compiler_params=params(),
        )(qg, qg_other, kv_blocks[j], *earlier)
    merged = scored[arrivals[-1]][3]
    merged_other = partner_swap(merged, count)

    dkv_shape = jax.ShapeDtypeStruct((rows, 2 * head), jnp.bfloat16)
    half_square = jax.ShapeDtypeStruct((rows, 2 * width), jnp.bfloat16)
    returned, dscores = {}, {}
    for j in steps:
        dkv_part, dscores[j] = pl.pallas_call(
            functools.partial(far_grad_kernel, group, rows, head),
            out_shape=(dkv_shape, half_square),
            in_specs=[vmem_spec()] * 7,
            out_specs=(vmem_spec(),) * 2,
            compiler_params=params(),
        )(*scored[j][0:3], merged, merged_other, qg, qg_other)
        returned[j] = chip_return(dkv_part, count, j)
    dkv_own, dq_own, dq_other = pl.pallas_call(
        functools.partial(near_grad_kernel, blocks, group, rows, head),
        out_shape=(
            jax.ShapeDtypeStruct((rows, 2 * head), jnp.float32),
            jax.ShapeDtypeStruct((rows, group * head), jnp.float32),
            jax.ShapeDtypeStruct((rows, group * head), jnp.bfloat16),
        ),
        in_specs=[vmem_spec()] * (6 + 2 * blocks),
        out_specs=(vmem_spec(),) * 3,
        scratch_shapes=[pltpu.VMEM((rows, 2 * width), jnp.bfloat16)],
        compiler_params=params(),
        name="grads0",
    )(
        *scored[0][0:3],
        merged,
        merged_other,
        qg,
        qg_other,
        kv,
        *(kv_blocks[j] for j in steps),
        *(dscores[j] for j in steps),
    )
    back = [(i, (i - 1) % sections) for i in range(sections)]
    dq_swapped = partner_swap(dq_other, count)
    dq = (dq_own + dq_swapped.astype(jnp.float32)).astype(jnp.bfloat16)
    dq_message = lax.ppermute(dq, "section", back)
    dkv = dkv_own
    for j in steps:
        dkv = dkv + returned[j].astype(jnp.float32)
    dkv_message = lax.ppermute(dkv.astype(jnp.bfloat16), "section", back)
    return jnp.concatenate([dq_message, dkv_message], axis=1)[None]


def send_order(count):
    return list(reversed(range(1, count // 2)))


def arrival_order(count):
    half = count // 4
    return [j for j in send_order(count) if j != half] + [half]


def solution(mesh):
    in_specs = (
        P("section", None, "ctx", None),
        P("section", None, "ctx", None),
        P("section", None, "ctx", None),
        P("section", "ctx", None),
        P("ctx"),
        P("section"),
    )
    out_specs = P("section", "ctx", None)

    return jax.shard_map(
        per_device, mesh=mesh, in_specs=in_specs, out_specs=out_specs, check_vma=False
    )
```

profile of v0, /device:TPU:0, one launch (start us, length us, event | category | flops | bytes accessed | tf_op | source)
XLA Modules:
  0.0 32.5 jit_solution(6839112449949002591)
XLA Ops:
  0.7 1.0 %fetch.1 = (bf16[136,256]{1,0:T(8,128)(2,1)S(1)}, bf16[1032,128]{1,0:T(8,128)(2,1)S(1)}) custom-call(s32[1]{0:T(128)S(6)} %copy.7.slot_ref, s32[2]{0:T(128)} %ids_ref.1, bf16[1,8,128,512]{3,2,1,0:T(8,128)(2,1)} %query_ref.1, bf16[1,8,128,128]{3,2,1,0:T(8,128)(2,1)} %key_ref.1, bf16[1,8,128,128]{3,2,1,0:T(8,128)(2,1)} %value_ref.1, bf16[1,128,512]{2,1,0:T(8,128)(2,1)} %grad_ref.1), custom_call_target="tpu_custom_call" | custom-call | tf_op jit(solution)/shard_map/fetch/pallas_call | solution.py:212
  1.7 0.6 %collective-permute-start = (bf16[1032,128]{1,0:T(8,128)(2,1)S(1)}, bf16[1032,128]{1,0:T(8,128)(2,1)S(1)}, u32[]{:S(2)}, u32[]{:S(2)}) collective-permute-start(bf16[1032,128]{1,0:T(8,128)(2,1)S(1)} %get-tuple-element.29.refs_0_.refs_5_), channel_id=1, source_target_pairs={{0,1},{1,0},{2,3},{3,2},{4,5},{5,4},{6,7},{7,6},{8,9},{9,8},{10,11... | collective-permute-start | bytes 792584 | tf_op jit(solution)/shard_map/ppermute | solution.py:32
  2.2 2.6 %collective-permute-start.3 = (bf16[136,256]{1,0:T(8,128)(2,1)S(1)}, bf16[136,256]{1,0:T(8,128)(2,1)S(1)}, u32[]{:S(2)}, u32[]{:S(2)}) collective-permute-start(bf16[136,256]{1,0:T(8,128)(2,1)S(1)} %get-tuple-element.30.refs_2_.refs_7_), channel_id=1, source_target_pairs={{0,2},{1,3},{2,0},{3,1},{4,6},{5,7},{6,4},{7,5},{8,10},{9,11},{10,... | collective-permute-start | bytes 208904 | tf_op jit(solution)/shard_map/ppermute | solution.py:45
  4.9 2.5 %collective-permute-start.2 = (bf16[136,256]{1,0:T(8,128)(2,1)S(1)}, bf16[136,256]{1,0:T(8,128)(2,1)S(1)}, u32[]{:S(2)}, u32[]{:S(2)}) collective-permute-start(bf16[136,256]{1,0:T(8,128)(2,1)S(1)} %get-tuple-element.30.refs_2_.refs_7_), channel_id=1, source_target_pairs={{0,6},{1,7},{2,4},{3,5},{4,2},{5,3},{6,0},{7,1},{8,14},{9,15},{10,... | collective-permute-start | bytes 208904 | tf_op jit(solution)/shard_map/ppermute | solution.py:45
  7.3 0.1 collective-permute-start.1
  7.5 0.0 collective-permute-done.refs_1_.refs_6_
  7.5 0.4 %shard_map.64 = (f32[128,1024]{1,0:T(8,128)S(1)}, f32[128,1024]{1,0:T(8,128)S(1)}, f32[8,1024]{1,0:T(8,128)S(1)}) custom-call(bf16[1032,128]{1,0:T(8,128)(2,1)S(1)} %get-tuple-element.29.refs_0_.refs_5_, bf16[1032,128]{1,0:T(8,128)(2,1)S(1)} %collective-permute-done.refs_1_.refs_6_, bf16[136,256]{1,0:T(8,128)(2,1)S(1)} %get-tuple-element.30.refs_2_.refs_7_), custom_call_target="tpu_custom_call" | custom-call | tf_op jit(solution)/shard_map/pallas_call | solution.py:241
  7.8 0.0 collective-permute-done.3.refs_2_.refs_10_
  7.8 0.4 %shard_map.66 = (f32[128,1024]{1,0:T(8,128)S(1)}, f32[128,1024]{1,0:T(8,128)S(1)}, f32[8,1024]{1,0:T(8,128)S(1)}) custom-call(bf16[1032,128]{1,0:T(8,128)(2,1)S(1)} %get-tuple-element.29.refs_0_.refs_5_, bf16[1032,128]{1,0:T(8,128)(2,1)S(1)} %collective-permute-done.refs_1_.refs_6_, bf16[136,256]{1,0:T(8,128)(2,1)S(1)} %collective-permute-done.3.refs_2_.refs_10_), custom_call_target="tpu_custom_call" | custom-call | tf_op jit(solution)/shard_map/pallas_call | solution.py:241
  8.2 3.6 %collective-permute-done.2.refs_2_.refs_8_ = bf16[136,256]{1,0:T(8,128)(2,1)S(1)} collective-permute-done((bf16[136,256]{1,0:T(8,128)(2,1)S(1)}, bf16[136,256]{1,0:T(8,128)(2,1)S(1)}, u32[]{:S(2)}, u32[]{:S(2)}) %collective-permute-start.2) | collective-permute-done | bytes 69664 | tf_op jit(solution)/shard_map/ppermute | solution.py:45
  11.8 0.4 %shard_map.65 = (f32[128,1024]{1,0:T(8,128)S(1)}, f32[128,1024]{1,0:T(8,128)S(1)}, f32[8,1024]{1,0:T(8,128)S(1)}) custom-call(bf16[1032,128]{1,0:T(8,128)(2,1)S(1)} %get-tuple-element.29.refs_0_.refs_5_, bf16[1032,128]{1,0:T(8,128)(2,1)S(1)} %collective-permute-done.refs_1_.refs_6_, bf16[136,256]{1,0:T(8,128)(2,1)S(1)} %collective-permute-done.2.refs_2_.refs_8_), custom_call_target="tpu_custom_call" | custom-call | tf_op jit(solution)/shard_map/pallas_call | solution.py:241
  12.2 2.2 %collective-permute-done.1.refs_2_.refs_9_ = bf16[136,256]{1,0:T(8,128)(2,1)S(1)} collective-permute-done((bf16[136,256]{1,0:T(8,128)(2,1)S(1)}, bf16[136,256]{1,0:T(8,128)(2,1)S(1)}, u32[]{:S(2)}, u32[]{:S(2)}) %collective-permute-start.1) | collective-permute-done | bytes 69664 | tf_op jit(solution)/shard_map/ppermute | solution.py:45
  14.4 0.4 %shard_map.67 = (f32[128,1024]{1,0:T(8,128)S(1)}, f32[128,1024]{1,0:T(8,128)S(1)}, f32[8,1024]{1,0:T(8,128)S(1)}, f32[8,1024]{1,0:T(8,128)S(1)}) custom-call(bf16[1032,128]{1,0:T(8,128)(2,1)S(1)} %get-tuple-element.29.refs_0_.refs_5_, bf16[1032,128]{1,0:T(8,128)(2,1)S(1)} %collective-permute-done.refs_1_.refs_6_, ...), custom_call_target="tpu_custom_call" | custom-call | tf_op jit(solution)/shard_map/pallas_call | solution.py:241
  14.9 0.2 collective-permute-start.4
  15.0 1.1 %collective-permute-done.4.refs_4_ = f32[8,1024]{1,0:T(8,128)S(1)} collective-permute-done((f32[8,1024]{1,0:T(8,128)S(1)}, f32[8,1024]{1,0:T(8,128)S(1)}, u32[]{:S(2)}, u32[]{:S(2)}) %collective-permute-start.4) | collective-permute-done | bytes 32800 | tf_op jit(solution)/shard_map/ppermute | solution.py:32
  16.1 0.3 shard_map.70
  16.5 0.3 shard_map.68
  16.8 0.3 shard_map.69
  17.1 0.7 %grads0.1 = (f32[128,256]{1,0:T(8,128)S(1)}, f32[128,512]{1,0:T(8,128)S(1)}, bf16[128,512]{1,0:T(8,128)(2,1)S(1)}) custom-call(f32[128,1024]{1,0:T(8,128)S(1)} %get-tuple-element.31.refs_0_, f32[128,1024]{1,0:T(8,128)S(1)} %get-tuple-element.32.refs_1_, f32[8,1024]{1,0:T(8,128)S(1)} %get-tuple-element.33.refs_3_.refs_2_, ...), custom_call_target="tpu_custom_call" | custom-call | tf_op jit(solution)/shard_map/grads0/pallas_call | solution.py:263
  17.8 0.2 collective-permute-start.5
  18.0 0.0 collective-permute-start.9
  18.0 3.2 %collective-permute-start.8 = (bf16[128,256]{1,0:T(8,128)(2,1)S(1)}, bf16[128,256]{1,0:T(8,128)(2,1)S(1)}, u32[]{:S(2)}, u32[]{:S(2)}) collective-permute-start(bf16[128,256]{1,0:T(8,128)(2,1)S(1)} %get-tuple-element.51), channel_id=1, source_target_pairs={{4,0},{5,1},{6,2},{7,3},{0,4},{1,5},{2,6},{3,7},{12,8},{13,9},{14,... | collective-permute-start | bytes 196616 | tf_op jit(solution)/shard_map/ppermute | solution.py:49
  21.3 1.1 %collective-permute-start.7 = (bf16[128,256]{1,0:T(8,128)(2,1)S(1)}, bf16[128,256]{1,0:T(8,128)(2,1)S(1)}, u32[]{:S(2)}, u32[]{:S(2)}) collective-permute-start(bf16[128,256]{1,0:T(8,128)(2,1)S(1)} %get-tuple-element.50), channel_id=1, source_target_pairs={{6,0},{7,1},{4,2},{5,3},{2,4},{3,5},{0,6},{1,7},{14,8},{15,9},{12,... | collective-permute-start | bytes 196616 | tf_op jit(solution)/shard_map/ppermute | solution.py:49
  22.4 0.0 collective-permute-done.5
  22.5 2.5 %collective-permute-start.6 = (bf16[128,512]{1,0:T(8,128)(2,1)S(1)}, bf16[128,512]{1,0:T(8,128)(2,1)S(1)}, u32[]{:S(2)}, u32[]{:S(2)}) collective-permute-start(bf16[128,512]{1,0:T(8,128)(2,1)S(1)} %add_convert_fusion), channel_id=1, source_target_pairs={{0,24},{8,0},{16,8},{24,16},{1,25},{9,1},{17,9},{25,17},{2,26},{10... | collective-permute-start | bytes 393224 | tf_op jit(solution)/shard_map/ppermute | solution.py:288
  25.0 0.0 collective-permute-done.9
  25.0 0.4 %collective-permute-done.8 = bf16[128,256]{1,0:T(8,128)(2,1)S(1)} collective-permute-done((bf16[128,256]{1,0:T(8,128)(2,1)S(1)}, bf16[128,256]{1,0:T(8,128)(2,1)S(1)}, u32[]{:S(2)}, u32[]{:S(2)}) %collective-permute-start.8) | collective-permute-done | bytes 65568 | tf_op jit(solution)/shard_map/ppermute | solution.py:49
  25.4 2.0 %collective-permute-done.7 = bf16[128,256]{1,0:T(8,128)(2,1)S(1)} collective-permute-done((bf16[128,256]{1,0:T(8,128)(2,1)S(1)}, bf16[128,256]{1,0:T(8,128)(2,1)S(1)}, u32[]{:S(2)}, u32[]{:S(2)}) %collective-permute-start.7) | collective-permute-done | bytes 65568 | tf_op jit(solution)/shard_map/ppermute | solution.py:49
  27.4 2.5 %collective-permute-start.10 = (bf16[128,256]{1,0:T(8,128)(2,1)S(1)}, bf16[128,256]{1,0:T(8,128)(2,1)S(1)}, u32[]{:S(2)}, u32[]{:S(2)}) collective-permute-start(bf16[128,256]{1,0:T(8,128)(2,1)S(1)} %add_convert_fusion.1), channel_id=1, source_target_pairs={{0,24},{8,0},{16,8},{24,16},{1,25},{9,1},{17,9},{25,17},{2,26},{10... | collective-permute-start | bytes 196616 | tf_op jit(solution)/shard_map/ppermute | solution.py:292
  29.9 1.9 %collective-permute-done.10 = bf16[128,256]{1,0:T(8,128)(2,1)S(1)} collective-permute-done((bf16[128,256]{1,0:T(8,128)(2,1)S(1)}, bf16[128,256]{1,0:T(8,128)(2,1)S(1)}, u32[]{:S(2)}, u32[]{:S(2)}) %collective-permute-start.10) | collective-permute-done | bytes 65568 | tf_op jit(solution)/shard_map/ppermute | solution.py:292
  31.8 0.0 collective-permute-done.6
  31.8 0.7 %maximum_bitcast_fusion = bf16[1,128,768]{2,1,0:T(8,128)(2,1)} fusion(bf16[128,256]{1,0:T(8,128)(2,1)S(1)} %collective-permute-done.10, bf16[128,512]{1,0:T(8,128)(2,1)S(1)} %collective-permute-done.6), kind=kLoop, calls=%fused_computation.1 | loop fusion | flops 393216 | bytes 393216 | tf_op jit(solution)/shard_map/broadcast_in_dim | solution.py:293
  (2 shorter events, 0.1 us)
Async XLA Ops:
  1.7 5.8 %collective-permute-start = (bf16[1032,128]{1,0:T(8,128)(2,1)S(1)}, bf16[1032,128]{1,0:T(8,128)(2,1)S(1)}, u32[]{:S(2)}, u32[]{:S(2)}) collective-permute-start(bf16[1032,128]{1,0:T(8,128)(2,1)S(1)} %get-tuple-element.29.refs_0_.refs_5_), channel_id=1, source_target_pairs={{0,1},{1,0},{2,3},{3,2},{4,5},{5,4},{6,7},{7,6},{8,9},{9,8},{10,11... | collective-permute-start | bytes 792584 | tf_op jit(solution)/shard_map/ppermute | solution.py:32
  2.2 5.6 %collective-permute-start.3 = (bf16[136,256]{1,0:T(8,128)(2,1)S(1)}, bf16[136,256]{1,0:T(8,128)(2,1)S(1)}, u32[]{:S(2)}, u32[]{:S(2)}) collective-permute-start(bf16[136,256]{1,0:T(8,128)(2,1)S(1)} %get-tuple-element.30.refs_2_.refs_7_), channel_id=1, source_target_pairs={{0,2},{1,3},{2,0},{3,1},{4,6},{5,7},{6,4},{7,5},{8,10},{9,11},{10,... | collective-permute-start | bytes 208904 | tf_op jit(solution)/shard_map/ppermute | solution.py:45
  4.9 7.0 %collective-permute-start.2 = (bf16[136,256]{1,0:T(8,128)(2,1)S(1)}, bf16[136,256]{1,0:T(8,128)(2,1)S(1)}, u32[]{:S(2)}, u32[]{:S(2)}) collective-permute-start(bf16[136,256]{1,0:T(8,128)(2,1)S(1)} %get-tuple-element.30.refs_2_.refs_7_), channel_id=1, source_target_pairs={{0,6},{1,7},{2,4},{3,5},{4,2},{5,3},{6,0},{7,1},{8,14},{9,15},{10,... | collective-permute-start | bytes 208904 | tf_op jit(solution)/shard_map/ppermute | solution.py:45
  7.3 7.1 %collective-permute-start.1 = (bf16[136,256]{1,0:T(8,128)(2,1)S(1)}, bf16[136,256]{1,0:T(8,128)(2,1)S(1)}, u32[]{:S(2)}, u32[]{:S(2)}) collective-permute-start(bf16[136,256]{1,0:T(8,128)(2,1)S(1)} %get-tuple-element.30.refs_2_.refs_7_), channel_id=1, source_target_pairs={{0,4},{1,5},{2,6},{3,7},{4,0},{5,1},{6,2},{7,3},{8,12},{9,13},{10,... | collective-permute-start | bytes 208904 | tf_op jit(solution)/shard_map/ppermute | solution.py:45
  14.9 1.3 %collective-permute-start.4 = (f32[8,1024]{1,0:T(8,128)S(1)}, f32[8,1024]{1,0:T(8,128)S(1)}, u32[]{:S(2)}, u32[]{:S(2)}) collective-permute-start(f32[8,1024]{1,0:T(8,128)S(1)} %get-tuple-element.36.refs_3_), channel_id=1, source_target_pairs={{0,1},{1,0},{2,3},{3,2},{4,5},{5,4},{6,7},{7,6},{8,9},{9,8},{10,11... | collective-permute-start | bytes 98312 | tf_op jit(solution)/shard_map/ppermute | solution.py:32
  17.8 4.6 %collective-permute-start.5 = (bf16[128,512]{1,0:T(8,128)(2,1)S(1)}, bf16[128,512]{1,0:T(8,128)(2,1)S(1)}, u32[]{:S(2)}, u32[]{:S(2)}) collective-permute-start(bf16[128,512]{1,0:T(8,128)(2,1)S(1)} %get-tuple-element.48), channel_id=1, source_target_pairs={{0,1},{1,0},{2,3},{3,2},{4,5},{5,4},{6,7},{7,6},{8,9},{9,8},{10,11... | collective-permute-start | bytes 393224 | tf_op jit(solution)/shard_map/ppermute | solution.py:32
  18.0 6.9 %collective-permute-start.9 = (bf16[128,256]{1,0:T(8,128)(2,1)S(1)}, bf16[128,256]{1,0:T(8,128)(2,1)S(1)}, u32[]{:S(2)}, u32[]{:S(2)}) collective-permute-start(bf16[128,256]{1,0:T(8,128)(2,1)S(1)} %get-tuple-element.52), channel_id=1, source_target_pairs={{2,0},{3,1},{0,2},{1,3},{6,4},{7,5},{4,6},{5,7},{10,8},{11,9},{8,1... | collective-permute-start | bytes 196616 | tf_op jit(solution)/shard_map/ppermute | solution.py:49
  18.0 7.4 %collective-permute-start.8 = (bf16[128,256]{1,0:T(8,128)(2,1)S(1)}, bf16[128,256]{1,0:T(8,128)(2,1)S(1)}, u32[]{:S(2)}, u32[]{:S(2)}) collective-permute-start(bf16[128,256]{1,0:T(8,128)(2,1)S(1)} %get-tuple-element.51), channel_id=1, source_target_pairs={{4,0},{5,1},{6,2},{7,3},{0,4},{1,5},{2,6},{3,7},{12,8},{13,9},{14,... | collective-permute-start | bytes 196616 | tf_op jit(solution)/shard_map/ppermute | solution.py:49
  21.3 6.1 %collective-permute-start.7 = (bf16[128,256]{1,0:T(8,128)(2,1)S(1)}, bf16[128,256]{1,0:T(8,128)(2,1)S(1)}, u32[]{:S(2)}, u32[]{:S(2)}) collective-permute-start(bf16[128,256]{1,0:T(8,128)(2,1)S(1)} %get-tuple-element.50), channel_id=1, source_target_pairs={{6,0},{7,1},{4,2},{5,3},{2,4},{3,5},{0,6},{1,7},{14,8},{15,9},{12,... | collective-permute-start | bytes 196616 | tf_op jit(solution)/shard_map/ppermute | solution.py:49
  22.5 9.3 %collective-permute-start.6 = (bf16[128,512]{1,0:T(8,128)(2,1)S(1)}, bf16[128,512]{1,0:T(8,128)(2,1)S(1)}, u32[]{:S(2)}, u32[]{:S(2)}) collective-permute-start(bf16[128,512]{1,0:T(8,128)(2,1)S(1)} %add_convert_fusion), channel_id=1, source_target_pairs={{0,24},{8,0},{16,8},{24,16},{1,25},{9,1},{17,9},{25,17},{2,26},{10... | collective-permute-start | bytes 393224 | tf_op jit(solution)/shard_map/ppermute | solution.py:288
  27.4 4.4 %collective-permute-start.10 = (bf16[128,256]{1,0:T(8,128)(2,1)S(1)}, bf16[128,256]{1,0:T(8,128)(2,1)S(1)}, u32[]{:S(2)}, u32[]{:S(2)}) collective-permute-start(bf16[128,256]{1,0:T(8,128)(2,1)S(1)} %add_convert_fusion.1), channel_id=1, source_target_pairs={{0,24},{8,0},{16,8},{24,16},{1,25},{9,1},{17,9},{25,17},{2,26},{10... | collective-permute-start | bytes 196616 | tf_op jit(solution)/shard_map/ppermute | solution.py:292
where the time goes:
time: 32.7 us; the launch traced here: 32.5 us
  starting transfers between devices  15.6 us (48%)
  waiting for transfers between devices  11.2 us (34%)
  Pallas kernels  4.2 us (13%)
  other arithmetic  0.75 us (2%)
  between operations  0.74 us (2%)
    ppermute x3, waiting for transfers between devices, chip_send(): return lax.ppermute(value, 'ctx', chip_pairs(count, step))  5.83 us
    ppermute x3, starting transfers between devices, chip_send(): return lax.ppermute(value, 'ctx', chip_pairs(count, step))  5.23 us
    ppermute x3, starting transfers between devices, chip_return(): lax.ppermute(value, 'ctx', [(b, a) for a, b in chip_pairs(count, step)])  4.39 us
    ppermute x1, starting transfers between devices, per_device(): dq_message = lax.ppermute(dq, 'section', back)  2.51 us
    ppermute x1, starting transfers between devices, per_device(): dkv_message = lax.ppermute(dkv.astype(jnp.bfloat16), 'section', back)  2.5 us
    ppermute x3, waiting for transfers between devices, chip_return(): lax.ppermute(value, 'ctx', [(b, a) for a, b in chip_pairs(count, step)])  2.39 us
    ppermute x1, waiting for transfers between devices, per_device(): dkv_message = lax.ppermute(dkv.astype(jnp.bfloat16), 'section', back)  1.91 us
    pallas_call x4, Pallas kernels, per_device(): pl.pallas_call(functools.partial(score_kernel, group, rows, head, len(ear...  1.53 us
  transfers between devices with their start and end apart: 11, of which 6 were waited for; matrix products, arithmetic and copies ran while one was open for 0% of the time, Pallas kernels for 3%

commit v1 on v0

--- a/solution.py
+++ b/solution.py
@@ -49,34 +49,62 @@
     return lax.ppermute(value, "ctx", [(b, a) for a, b in chip_pairs(count, step)])
 
 
-def fetch_kernel(slot_ref, ids_ref, query_ref, key_ref, value_ref, grad_ref, kv_ref, qg_ref, ids, sems):
+def id_block(ids_ref, head):
+    row = lax.broadcasted_iota(jnp.int32, (ID_ROWS, head), 0)
+    chosen = jnp.where(row < ID_ROWS // 2, ids_ref[0], ids_ref[1])
+    return chosen.astype(jnp.float32).astype(jnp.bfloat16)
+
+
+def fetch_kv_kernel(slot_ref, ids_ref, key_ref, value_ref, kv_ref, ids, sems):
     rows, head = key_ref.shape[2:]
-    group = query_ref.shape[3] // head
     slot = slot_ref[0]
-    ids_copy = pltpu.make_async_copy(ids_ref, ids, sems.at[0])
     copies = [
-        pltpu.make_async_copy(key_ref.at[0, slot], kv_ref.at[0:rows, 0:head], sems.at[1]),
-        pltpu.make_async_copy(value_ref.at[0, slot], kv_ref.at[0:rows, head : 2 * head], sems.at[2]),
+        pltpu.make_async_copy(key_ref.at[0, slot], kv_ref.at[0:rows], sems.at[0]),
+        pltpu.make_async_copy(value_ref.at[0, slot], kv_ref.at[rows : 2 * rows], sems.at[1]),
     ]
+    ids_copy = pltpu.make_async_copy(ids_ref, ids, sems.at[2])
+    ids_copy.start()
+    for copy in copies:
+        copy.start()
+    ids_copy.wait()
+    kv_ref[2 * rows : 2 * rows + ID_ROWS, :] = id_block(ids, head)
+    for copy in copies:
+        copy.wait()
+
+
+def fetch_qg_kernel(slot_ref, query_ref, grad_ref, kv_ref, qg_ref, sems):
+    rows, width = query_ref.shape[2:]
+    head = kv_ref.shape[1]
+    group = width // head
+    slot = slot_ref[0]
+    copies = []
     for h in range(group):
         cols = slice(h * head, (h + 1) * head)
         query_to = qg_ref.at[h * rows : (h + 1) * rows]
         grad_to = qg_ref.at[(group + h) * rows : (group + h + 1) * rows]
         copies.append(
-            pltpu.make_async_copy(query_ref.at[0, slot, :, cols], query_to, sems.at[3 + 2 * h])
+            pltpu.make_async_copy(query_ref.at[0, slot, :, cols], query_to, sems.at[2 * h])
         )
-        copies.append(pltpu.make_async_copy(grad_ref.at[0, :, cols], grad_to, sems.at[4 + 2 * h]))
-    ids_copy.start()
+        copies.append(pltpu.make_async_copy(grad_ref.at[0, :, cols], grad_to, sems.at[2 * h + 1]))
     for copy in copies:
         copy.start()
-    ids_copy.wait()
-    half = ID_ROWS // 2
-    row = lax.broadcasted_iota(jnp.int32, (ID_ROWS, 2 * head), 0)
-    lines = jnp.where(row < half, ids[0], ids[1]).astype(jnp.float32).astype(jnp.bfloat16)
-    kv_ref[rows : rows + ID_ROWS, :] = lines
-    qg_ref[2 * group * rows : 2 * group * rows + ID_ROWS, :] = lines[:, 0:head]
+    last = 2 * group * rows
+    qg_ref[last : last + ID_ROWS, :] = kv_ref[2 * rows : 2 * rows + ID_ROWS, :]
     for copy in copies:
         copy.wait()
+
+
+def write_dq_kernel(dq_ref, out_ref, sem):
+    copy = pltpu.make_async_copy(dq_ref, out_ref.at[0, :, 0 : dq_ref.shape[1]], sem)
+    copy.start()
+    copy.wait()
+
+
+def write_dkv_kernel(filled_ref, dkv_ref, out_ref, sem):
+    start = out_ref.shape[2] - dkv_ref.shape[1]
+    copy = pltpu.make_async_copy(dkv_ref, out_ref.at[0, :, start : out_ref.shape[2]], sem)
+    copy.start()
+    copy.wait()
 
 
 def id_lines(ref, start, width):
@@ -115,8 +143,8 @@
     stretch = rows // 2
     scale = LOG2E / math.sqrt(head)
     in_stretch = lax.broadcasted_iota(jnp.int32, (stretch, 1), 0).astype(jnp.float32)
-    ids = id_lines(kv_ref, rows, head)
-    key, value = kv_ref[0:rows, 0:head], kv_ref[0:rows, head : 2 * head]
+    ids = id_lines(kv_ref, 2 * rows, head)
+    key, value = kv_ref[0:rows, :], kv_ref[rows : 2 * rows, :]
     for b in range(2):
         lanes = slice(b * width, (b + 1) * width)
         place = lane_positions(qg_refs[b], group, rows, head)
@@ -149,23 +177,29 @@
         merged_ref[3:8, :] = jnp.zeros((5, 2 * width), jnp.float32)
 
 
-def block_grads(group, rows, head, refs, dkv_ref, dscore_ref):
-    exp_ref, dprob_ref, stat_ref, merged_ref, other_ref = refs[0:5]
-    qg_refs = refs[5:7]
+def half_weights(refs, lanes, swapped):
+    exp_ref, dprob_ref, stat_ref, merged_ref, other_ref = refs
+    top, total, mixed = (merged_ref[i : i + 1, lanes] for i in range(3))
+    top_o, total_o, mixed_o = (other_ref[i : i + 1, swapped] for i in range(3))
+    high = jnp.maximum(top, top_o)
+    own, other = jnp.exp2(top - high), jnp.exp2(top_o - high)
+    inverse = 1.0 / (total * own + total_o * other)
+    delta = (mixed * own + mixed_o * other) * inverse
+    fade = jnp.exp2(stat_ref[0:1, lanes] - high) * inverse
+    probs = exp_ref[:, lanes] * fade
+    return probs, (probs * (dprob_ref[:, lanes] - delta)).astype(jnp.bfloat16)
+
+
+def half_lanes(b, width):
+    return slice(b * width, (b + 1) * width), slice((1 - b) * width, (2 - b) * width)
+
+
+def block_grads(group, rows, head, refs, qg_refs, dkv_ref, dscore_ref):
     width = group * rows
     dk = dv = None
     for b in range(2):
-        lanes = slice(b * width, (b + 1) * width)
-        swapped = slice((1 - b) * width, (2 - b) * width)
-        top, total, mixed = (merged_ref[i : i + 1, lanes] for i in range(3))
-        top_o, total_o, mixed_o = (other_ref[i : i + 1, swapped] for i in range(3))
-        high = jnp.maximum(top, top_o)
-        own, other = jnp.exp2(top - high), jnp.exp2(top_o - high)
-        inverse = 1.0 / (total * own + total_o * other)
-        delta = (mixed * own + mixed_o * other) * inverse
-        fade = jnp.exp2(stat_ref[0:1, lanes] - high) * inverse
-        probs = exp_ref[:, lanes] * fade
-        dscore = (probs * (dprob_ref[:, lanes] - delta)).astype(jnp.bfloat16)
+        lanes, swapped = half_lanes(b, width)
+        probs, dscore = half_weights(refs, lanes, swapped)
         dscore_ref[:, lanes] = dscore
         dk_part = dot_nn(dscore, qg_refs[b][0:width, :])
         dv_part = dot_nn(probs.astype(jnp.bfloat16), qg_refs[b][width : 2 * width, :])
@@ -175,26 +209,35 @@
     dkv_ref[:, head : 2 * head] = dv.astype(dkv_ref.dtype)
 
 
+def half_query_grad(group, rows, head, kv_refs, dscores, dq_ref):
+    dq = None
+    for kv_ref, dscore in zip(kv_refs, dscores):
+        part = dot_tn(kv_ref[0:rows, :], dscore)
+        dq = part if dq is None else dq + part
+    for h in range(group):
+        piece = jnp.transpose(dq[:, h * rows : (h + 1) * rows]) * (1.0 / math.sqrt(head))
+        dq_ref[:, h * head : (h + 1) * head] = piece.astype(dq_ref.dtype)
+
+
 def far_grad_kernel(group, rows, head, *refs):
-    block_grads(group, rows, head, refs[0:7], refs[7], refs[8])
+    block_grads(group, rows, head, refs[0:5], refs[5:7], refs[7], refs[8])
+
+
+def other_query_grad_kernel(blocks, group, rows, head, *refs):
+    lanes, swapped = half_lanes(1, group * rows)
+    kv_refs = refs[5 : 5 + blocks]
+    near = half_weights(refs[0:5], lanes, swapped)[1]
+    far = [ref[:, lanes] for ref in refs[5 + blocks : 4 + 2 * blocks]]
+    half_query_grad(group, rows, head, kv_refs, [near] + far, refs[4 + 2 * blocks])
 
 
 def near_grad_kernel(blocks, group, rows, head, *refs):
+    lanes = slice(0, group * rows)
     kv_refs = refs[7 : 7 + blocks]
-    dscore_refs = refs[7 + blocks : 6 + 2 * blocks]
-    dkv_ref, dq_own_ref, dq_other_ref, dscore_ref = refs[6 + 2 * blocks :]
-    width = group * rows
-    scale = 1.0 / math.sqrt(head)
-    block_grads(group, rows, head, refs[0:7], dkv_ref, dscore_ref)
-    for b, dq_ref in enumerate((dq_own_ref, dq_other_ref)):
-        lanes = slice(b * width, (b + 1) * width)
-        dq = None
-        for kv_ref, ref in zip(kv_refs, (dscore_ref,) + tuple(dscore_refs)):
-            part = dot_tn(kv_ref[0:rows, 0:head], ref[:, lanes])
-            dq = part if dq is None else dq + part
-        for h in range(group):
-            piece = jnp.transpose(dq[:, h * rows : (h + 1) * rows]) * scale
-            dq_ref[:, h * head : (h + 1) * head] = piece.astype(dq_ref.dtype)
+    dkv_ref, dq_ref, dscore_ref = refs[6 + 2 * blocks :]
+    block_grads(group, rows, head, refs[0:5], refs[5:7], dkv_ref, dscore_ref)
+    dscores = [dscore_ref[:, lanes]] + [ref[:, lanes] for ref in refs[7 + blocks : 6 + 2 * blocks]]
+    half_query_grad(group, rows, head, kv_refs, dscores, dq_ref)
 
 
 def params():
@@ -209,21 +252,25 @@
     blocks = count // 2
     sections = lax.axis_size("section")
 
-    kv, qg = pl.pallas_call(
-        fetch_kernel,
-        out_shape=(
-            jax.ShapeDtypeStruct((rows + ID_ROWS, 2 * head), jnp.bfloat16),
-            jax.ShapeDtypeStruct((2 * width + ID_ROWS, head), jnp.bfloat16),
-        ),
-        in_specs=[pl.BlockSpec(memory_space=pltpu.SMEM)] + [hbm_spec()] * 5,
-        out_specs=(vmem_spec(), vmem_spec()),
-        scratch_shapes=[
-            pltpu.SMEM(stretch_ids.shape, jnp.int32),
-            pltpu.SemaphoreType.DMA((3 + 2 * group,)),
-        ],
-        compiler_params=params(),
-        name="fetch",
-    )(stash_slot, *(in_hbm(x) for x in (stretch_ids, queries, keys, values, out_grad)))
+    in_smem = pl.BlockSpec(memory_space=pltpu.SMEM)
+    kv = pl.pallas_call(
+        fetch_kv_kernel,
+        out_shape=jax.ShapeDtypeStruct((2 * rows + ID_ROWS, head), jnp.bfloat16),
+        in_specs=[in_smem] + [hbm_spec()] * 3,
+        out_specs=vmem_spec(),
+        scratch_shapes=[pltpu.SMEM(stretch_ids.shape, jnp.int32), pltpu.SemaphoreType.DMA((3,))],
+        compiler_params=params(),
+        name="fetch_kv",
+    )(stash_slot, in_hbm(stretch_ids), in_hbm(keys), in_hbm(values))
+    qg = pl.pallas_call(
+        fetch_qg_kernel,
+        out_shape=jax.ShapeDtypeStruct((2 * width + ID_ROWS, head), jnp.bfloat16),
+        in_specs=[in_smem] + [hbm_spec()] * 2 + [vmem_spec()],
+        out_specs=vmem_spec(),
+        scratch_shapes=[pltpu.SemaphoreType.DMA((2 * group,))],
+        compiler_params=params(),
+        name="fetch_qg",
+    )(stash_slot, in_hbm(queries), in_hbm(out_grad), kv)
 
     steps = send_order(count)
     arrivals = arrival_order(count)
@@ -260,37 +307,56 @@
             compiler_params=params(),
         )(*scored[j][0:3], merged, merged_other, qg, qg_other)
         returned[j] = chip_return(dkv_part, count, j)
-    dkv_own, dq_own, dq_other = pl.pallas_call(
+    near = (*scored[0][0:3], merged, merged_other)
+    shared = (kv, *(kv_blocks[j] for j in steps), *(dscores[j] for j in steps))
+    dq_other = pl.pallas_call(
+        functools.partial(other_query_grad_kernel, blocks, group, rows, head),
+        out_shape=jax.ShapeDtypeStruct((rows, group * head), jnp.bfloat16),
+        in_specs=[vmem_spec()] * (4 + 2 * blocks),
+        out_specs=vmem_spec(),
+        compiler_params=params(),
+        name="dq_other",
+    )(*near, *shared)
+    dq_swapped = partner_swap(dq_other, count)
+    dkv_own, dq_own = pl.pallas_call(
         functools.partial(near_grad_kernel, blocks, group, rows, head),
         out_shape=(
             jax.ShapeDtypeStruct((rows, 2 * head), jnp.float32),
             jax.ShapeDtypeStruct((rows, group * head), jnp.float32),
-            jax.ShapeDtypeStruct((rows, group * head), jnp.bfloat16),
         ),
         in_specs=[vmem_spec()] * (6 + 2 * blocks),
-        out_specs=(vmem_spec(),) * 3,
+        out_specs=(vmem_spec(),) * 2,
         scratch_shapes=[pltpu.VMEM((rows, 2 * width), jnp.bfloat16)],
         compiler_params=params(),
         name="grads0",
-    )(
-        *scored[0][0:3],
-        merged,
-        merged_other,
-        qg,
-        qg_other,
-        kv,
-        *(kv_blocks[j] for j in steps),
-        *(dscores[j] for j in steps),
-    )
+    )(*near, qg, qg_other, *shared)
     back = [(i, (i - 1) % sections) for i in range(sections)]
-    dq_swapped = partner_swap(dq_other, count)
     dq = (dq_own + dq_swapped.astype(jnp.float32)).astype(jnp.bfloat16)
     dq_message = lax.ppermute(dq, "section", back)
     dkv = dkv_own
     for j in steps:
         dkv = dkv + returned[j].astype(jnp.float32)
     dkv_message = lax.ppermute(dkv.astype(jnp.bfloat16), "section", back)
-    return jnp.concatenate([dq_message, dkv_message], axis=1)[None]
+    out_shape = jax.ShapeDtypeStruct((1, rows, width // rows * head + 2 * head), jnp.bfloat16)
+    filled = pl.pallas_call(
+        write_dq_kernel,
+        out_shape=out_shape,
+        in_specs=[vmem_spec()],
+        out_specs=hbm_spec(),
+        scratch_shapes=[pltpu.SemaphoreType.DMA],
+        compiler_params=params(),
+        name="write_dq",
+    )(dq_message)
+    return pl.pallas_call(
+        write_dkv_kernel,
+        out_shape=out_shape,
+        in_specs=[hbm_spec(), vmem_spec()],
+        out_specs=hbm_spec(),
+        scratch_shapes=[pltpu.SemaphoreType.DMA],
+        input_output_aliases={0: 0},
+        compiler_params=params(),
+        name="write_dkv",
+    )(filled, dkv_message)
 
 
 def send_order(count):

time: 32.7 us -> 33.1 us (1.012)
  Pallas kernels: 4.2 us -> 6.55 us
  waiting for transfers between devices: 11.2 us -> 9.84 us
  other arithmetic: 0.75 us -> 0.07 us
    pallas_call x1 -> x5, Pallas kernels: 1.01 us -> 3.48 us  [the longest x1 0.95 us: per_device(): pl.pallas_call(fetch_qg_kernel, out_shape=jax.ShapeDtypeStruct((2 * width...]
    broadcast_in_dim x1 -> x0, other arithmetic: 0.69 us -> none  [per_device(): return jnp.concatenate([dq_message, dkv_message], axis=1)[None]]
    ppermute x1, waiting for transfers between devices: 1.91 us -> 1.23 us  [per_device(): dkv_message = lax.ppermute(dkv.astype(jnp.bfloat16), 'section', back)]
    ppermute x3, waiting for transfers between devices: 2.39 us -> 1.83 us  [chip_return(): lax.ppermute(value, 'ctx', [(b, a) for a, b in chip_pairs(count, step)])]
  transfers between devices with their start and end apart: 11 -> 11, of which waited for: 6 -> 5; matrix products, arithmetic and copies ran while one was open for 0% -> 0% of each run, Pallas kernels for 3% -> 7%
where the time goes in v1:
time: 33.1 us; the launch traced here: 32.8 us
  starting transfers between devices  15.6 us (47%)
  waiting for transfers between devices  9.84 us (30%)
  Pallas kernels  6.55 us (20%)
  between operations  0.77 us (2%)
    ppermute x3, waiting for transfers between devices, chip_send(): return lax.ppermute(value, 'ctx', chip_pairs(count, step))  5.65 us
    ppermute x3, starting transfers between devices, chip_send(): return lax.ppermute(value, 'ctx', chip_pairs(count, step))  5.23 us
    ppermute x3, starting transfers between devices, chip_return(): lax.ppermute(value, 'ctx', [(b, a) for a, b in chip_pairs(count, step)])  4.39 us
    ppermute x1, starting transfers between devices, per_device(): dkv_message = lax.ppermute(dkv.astype(jnp.bfloat16), 'section', back)  2.51 us
    ppermute x1, starting transfers between devices, per_device(): dq_message = lax.ppermute(dq, 'section', back)  2.5 us
    ppermute x3, waiting for transfers between devices, chip_return(): lax.ppermute(value, 'ctx', [(b, a) for a, b in chip_pairs(count, step)])  1.83 us
    pallas_call x4, Pallas kernels, per_device(): pl.pallas_call(functools.partial(score_kernel, group, rows, head, len(ear...  1.54 us
    ppermute x1, waiting for transfers between devices, per_device(): dkv_message = lax.ppermute(dkv.astype(jnp.bfloat16), 'section', back)  1.23 us
  transfers between devices with their start and end apart: 11, of which 5 were waited for; matrix products, arithmetic and copies ran while one was open for 0% of the time, Pallas kernels for 7%

profile of v1, /device:TPU:0, one launch (start us, length us, event | category | flops | bytes accessed | tf_op | source)
XLA Modules:
  0.0 32.8 jit_solution(3033411041002262379)
XLA Ops:
  0.7 0.8 %fetch_kv.1.kv_ref.refs_2_.refs_7_.refs_5_ = bf16[264,128]{1,0:T(8,128)(2,1)S(1)} custom-call(s32[1]{0:T(128)S(6)} %copy.9.slot_ref, s32[2]{0:T(128)} %ids_ref.1, bf16[1,8,128,128]{3,2,1,0:T(8,128)(2,1)} %key_ref.1, bf16[1,8,128,128]{3,2,1,0:T(8,128)(2,1)} %value_ref.1), custom_call_target="tpu_custom_call" | custom-call | tf_op jit(solution)/shard_map/fetch_kv/pallas_call | solution.py:256
  1.5 1.0 %fetch_qg.1.refs_0_.refs_5_ = bf16[1032,128]{1,0:T(8,128)(2,1)S(1)} custom-call(s32[1]{0:T(128)S(6)} %copy.9.slot_ref, bf16[1,8,128,512]{3,2,1,0:T(8,128)(2,1)} %query_ref.1, bf16[1,128,512]{2,1,0:T(8,128)(2,1)} %grad_ref.1, bf16[264,128]{1,0:T(8,128)(2,1)S(1)} %fetch_kv.1.kv_ref.refs_2_.refs_7_.refs_5_), custom_call_target="tpu_custom_call" | custom-call | tf_op jit(solution)/shard_map/fetch_qg/pallas_call | solution.py:265
  2.4 0.6 %collective-permute-start = (bf16[1032,128]{1,0:T(8,128)(2,1)S(1)}, bf16[1032,128]{1,0:T(8,128)(2,1)S(1)}, u32[]{:S(2)}, u32[]{:S(2)}) collective-permute-start(bf16[1032,128]{1,0:T(8,128)(2,1)S(1)} %fetch_qg.1.refs_0_.refs_5_), channel_id=1, source_target_pairs={{0,1},{1,0},{2,3},{3,2},{4,5},{5,4},{6,7},{7,6},{8,9},{9,8},{10,11... | collective-permute-start | bytes 792584 | tf_op jit(solution)/shard_map/ppermute | solution.py:32
  3.0 2.6 %collective-permute-start.3 = (bf16[264,128]{1,0:T(8,128)(2,1)S(1)}, bf16[264,128]{1,0:T(8,128)(2,1)S(1)}, u32[]{:S(2)}, u32[]{:S(2)}) collective-permute-start(bf16[264,128]{1,0:T(8,128)(2,1)S(1)} %fetch_kv.1.kv_ref.refs_2_.refs_7_.refs_5_), channel_id=1, source_target_pairs={{0,2},{1,3},{2,0},{3,1},{4,6},{5,7},{6,4},{7,5},{8,10},{9,11},{10,... | collective-permute-start | bytes 202760 | tf_op jit(solution)/shard_map/ppermute | solution.py:45
  5.6 2.5 %collective-permute-start.2 = (bf16[264,128]{1,0:T(8,128)(2,1)S(1)}, bf16[264,128]{1,0:T(8,128)(2,1)S(1)}, u32[]{:S(2)}, u32[]{:S(2)}) collective-permute-start(bf16[264,128]{1,0:T(8,128)(2,1)S(1)} %fetch_kv.1.kv_ref.refs_2_.refs_7_.refs_5_), channel_id=1, source_target_pairs={{0,6},{1,7},{2,4},{3,5},{4,2},{5,3},{6,0},{7,1},{8,14},{9,15},{10,... | collective-permute-start | bytes 202760 | tf_op jit(solution)/shard_map/ppermute | solution.py:45
  8.1 0.1 collective-permute-start.1
  8.2 0.0 collective-permute-done.refs_1_.refs_6_
  8.2 0.4 %shard_map.64 = (f32[128,1024]{1,0:T(8,128)S(1)}, f32[128,1024]{1,0:T(8,128)S(1)}, f32[8,1024]{1,0:T(8,128)S(1)}) custom-call(bf16[1032,128]{1,0:T(8,128)(2,1)S(1)} %fetch_qg.1.refs_0_.refs_5_, bf16[1032,128]{1,0:T(8,128)(2,1)S(1)} %collective-permute-done.refs_1_.refs_6_, bf16[264,128]{1,0:T(8,128)(2,1)S(1)} %fetch_kv.1.kv_ref.refs_2_.refs_7_.refs_5_), custom_call_target="tpu_custom_call" | custom-call | tf_op jit(solution)/shard_map/pallas_call | solution.py:288
  8.6 0.0 collective-permute-done.3.refs_2_.refs_10_.refs_8_
  8.6 0.4 %shard_map.66 = (f32[128,1024]{1,0:T(8,128)S(1)}, f32[128,1024]{1,0:T(8,128)S(1)}, f32[8,1024]{1,0:T(8,128)S(1)}) custom-call(bf16[1032,128]{1,0:T(8,128)(2,1)S(1)} %fetch_qg.1.refs_0_.refs_5_, bf16[1032,128]{1,0:T(8,128)(2,1)S(1)} %collective-permute-done.refs_1_.refs_6_, bf16[264,128]{1,0:T(8,128)(2,1)S(1)} %collective-permute-done.3.refs_2_.refs_10_.refs_8_), custom_call_target="tpu_custom_call" | custom-call | tf_op jit(solution)/shard_map/pallas_call | solution.py:288
  9.0 3.5 %collective-permute-done.2.refs_2_.refs_8_.refs_6_ = bf16[264,128]{1,0:T(8,128)(2,1)S(1)} collective-permute-done((bf16[264,128]{1,0:T(8,128)(2,1)S(1)}, bf16[264,128]{1,0:T(8,128)(2,1)S(1)}, u32[]{:S(2)}, u32[]{:S(2)}) %collective-permute-start.2) | collective-permute-done | bytes 67616 | tf_op jit(solution)/shard_map/ppermute | solution.py:45
  12.5 0.4 %shard_map.65 = (f32[128,1024]{1,0:T(8,128)S(1)}, f32[128,1024]{1,0:T(8,128)S(1)}, f32[8,1024]{1,0:T(8,128)S(1)}) custom-call(bf16[1032,128]{1,0:T(8,128)(2,1)S(1)} %fetch_qg.1.refs_0_.refs_5_, bf16[1032,128]{1,0:T(8,128)(2,1)S(1)} %collective-permute-done.refs_1_.refs_6_, bf16[264,128]{1,0:T(8,128)(2,1)S(1)} %collective-permute-done.2.refs_2_.refs_8_.refs_6_), custom_call_target="tpu_custom_call" | custom-call | tf_op jit(solution)/shard_map/pallas_call | solution.py:288
  12.9 2.1 %collective-permute-done.1.refs_2_.refs_9_.refs_7_ = bf16[264,128]{1,0:T(8,128)(2,1)S(1)} collective-permute-done((bf16[264,128]{1,0:T(8,128)(2,1)S(1)}, bf16[264,128]{1,0:T(8,128)(2,1)S(1)}, u32[]{:S(2)}, u32[]{:S(2)}) %collective-permute-start.1) | collective-permute-done | bytes 67616 | tf_op jit(solution)/shard_map/ppermute | solution.py:45
  15.0 0.4 %shard_map.67 = (f32[128,1024]{1,0:T(8,128)S(1)}, f32[128,1024]{1,0:T(8,128)S(1)}, f32[8,1024]{1,0:T(8,128)S(1)}, f32[8,1024]{1,0:T(8,128)S(1)}) custom-call(bf16[1032,128]{1,0:T(8,128)(2,1)S(1)} %fetch_qg.1.refs_0_.refs_5_, bf16[1032,128]{1,0:T(8,128)(2,1)S(1)} %collective-permute-done.refs_1_.refs_6_, ...), custom_call_target="tpu_custom_call" | custom-call | tf_op jit(solution)/shard_map/pallas_call | solution.py:288
  15.4 0.2 collective-permute-start.4
  15.6 1.1 %collective-permute-done.4.refs_4_ = f32[8,1024]{1,0:T(8,128)S(1)} collective-permute-done((f32[8,1024]{1,0:T(8,128)S(1)}, f32[8,1024]{1,0:T(8,128)S(1)}, u32[]{:S(2)}, u32[]{:S(2)}) %collective-permute-start.4) | collective-permute-done | bytes 32800 | tf_op jit(solution)/shard_map/ppermute | solution.py:32
  16.7 0.3 shard_map.70
  17.0 0.3 shard_map.68
  17.4 0.3 %shard_map.69 = (bf16[128,256]{1,0:T(8,128)(2,1)S(1)}, bf16[128,1024]{1,0:T(8,128)(2,1)S(1)}) custom-call(f32[128,1024]{1,0:T(8,128)S(1)} %get-tuple-element.35.refs_0_, f32[128,1024]{1,0:T(8,128)S(1)} %get-tuple-element.36.refs_1_, f32[8,1024]{1,0:T(8,128)S(1)} %get-tuple-element.37.refs_2_, f32[8,1024]{1,0:T(8,128)S(1)} %get-tuple-element.31.refs_3_, ...), custom_call_target="tpu_custom_call" | custom-call | tf_op jit(solution)/shard_map/pallas_call | solution.py:302
  17.7 0.4 %dq_other.1 = bf16[128,512]{1,0:T(8,128)(2,1)S(1)} custom-call(f32[128,1024]{1,0:T(8,128)S(1)} %get-tuple-element.26.refs_0_, f32[128,1024]{1,0:T(8,128)S(1)} %get-tuple-element.27.refs_1_, f32[8,1024]{1,0:T(8,128)S(1)} %get-tuple-element.28.refs_3_.refs_2_, f32[8,1024]{1,0:T(8,128)S(1)} %get-tuple-element.31.refs_3_, ...), custom_call_target="tpu_custom_call" | custom-call | tf_op jit(solution)/shard_map/dq_other/pallas_call | solution.py:312
  18.1 0.2 collective-permute-start.5
  18.4 0.0 collective-permute-start.9
  18.4 3.3 %collective-permute-start.8 = (bf16[128,256]{1,0:T(8,128)(2,1)S(1)}, bf16[128,256]{1,0:T(8,128)(2,1)S(1)}, u32[]{:S(2)}, u32[]{:S(2)}) collective-permute-start(bf16[128,256]{1,0:T(8,128)(2,1)S(1)} %get-tuple-element.45), channel_id=1, source_target_pairs={{4,0},{5,1},{6,2},{7,3},{0,4},{1,5},{2,6},{3,7},{12,8},{13,9},{14,... | collective-permute-start | bytes 196616 | tf_op jit(solution)/shard_map/ppermute | solution.py:49
  21.6 1.1 %collective-permute-start.7 = (bf16[128,256]{1,0:T(8,128)(2,1)S(1)}, bf16[128,256]{1,0:T(8,128)(2,1)S(1)}, u32[]{:S(2)}, u32[]{:S(2)}) collective-permute-start(bf16[128,256]{1,0:T(8,128)(2,1)S(1)} %get-tuple-element.44), channel_id=1, source_target_pairs={{6,0},{7,1},{4,2},{5,3},{2,4},{3,5},{0,6},{1,7},{14,8},{15,9},{12,... | collective-permute-start | bytes 196616 | tf_op jit(solution)/shard_map/ppermute | solution.py:49
  22.8 0.5 %grads0.1 = (f32[128,256]{1,0:T(8,128)S(1)}, f32[128,512]{1,0:T(8,128)S(1)}) custom-call(f32[128,1024]{1,0:T(8,128)S(1)} %get-tuple-element.26.refs_0_, f32[128,1024]{1,0:T(8,128)S(1)} %get-tuple-element.27.refs_1_, f32[8,1024]{1,0:T(8,128)S(1)} %get-tuple-element.28.refs_3_.refs_2_, f32[8,1024]{1,0:T(8,128)S(1)} %get-tuple-element.31.refs_3_, ...), custom_call_target="tpu_custom_call" | custom-call | tf_op jit(solution)/shard_map/grads0/pallas_call | solution.py:321
  23.3 0.0 collective-permute-done.5
  23.4 2.5 %collective-permute-start.6 = (bf16[128,512]{1,0:T(8,128)(2,1)S(1)}, bf16[128,512]{1,0:T(8,128)(2,1)S(1)}, u32[]{:S(2)}, u32[]{:S(2)}) collective-permute-start(bf16[128,512]{1,0:T(8,128)(2,1)S(1)} %add_convert_fusion), channel_id=1, source_target_pairs={{0,24},{8,0},{16,8},{24,16},{1,25},{9,1},{17,9},{25,17},{2,26},{10... | collective-permute-start | bytes 393224 | tf_op jit(solution)/shard_map/ppermute | solution.py:335
  25.9 0.0 collective-permute-done.9
  25.9 0.0 collective-permute-done.8
  25.9 1.8 %collective-permute-done.7 = bf16[128,256]{1,0:T(8,128)(2,1)S(1)} collective-permute-done((bf16[128,256]{1,0:T(8,128)(2,1)S(1)}, bf16[128,256]{1,0:T(8,128)(2,1)S(1)}, u32[]{:S(2)}, u32[]{:S(2)}) %collective-permute-start.7) | collective-permute-done | bytes 65568 | tf_op jit(solution)/shard_map/ppermute | solution.py:49
  27.7 2.5 %collective-permute-start.10 = (bf16[128,256]{1,0:T(8,128)(2,1)S(1)}, bf16[128,256]{1,0:T(8,128)(2,1)S(1)}, u32[]{:S(2)}, u32[]{:S(2)}) collective-permute-start(bf16[128,256]{1,0:T(8,128)(2,1)S(1)} %add_convert_fusion.1), channel_id=1, source_target_pairs={{0,24},{8,0},{16,8},{24,16},{1,25},{9,1},{17,9},{25,17},{2,26},{10... | collective-permute-start | bytes 196616 | tf_op jit(solution)/shard_map/ppermute | solution.py:339
  30.2 0.0 collective-permute-done.6.dq_ref
  30.2 0.7 %write_dq.1.filled_ref = bf16[1,128,768]{2,1,0:T(8,128)(2,1)} custom-call(bf16[128,512]{1,0:T(8,128)(2,1)S(1)} %collective-permute-done.6.dq_ref), custom_call_target="tpu_custom_call" | custom-call | tf_op jit(solution)/shard_map/write_dq/pallas_call | solution.py:341
  30.9 1.2 %collective-permute-done.10.dkv_ref = bf16[128,256]{1,0:T(8,128)(2,1)S(1)} collective-permute-done((bf16[128,256]{1,0:T(8,128)(2,1)S(1)}, bf16[128,256]{1,0:T(8,128)(2,1)S(1)}, u32[]{:S(2)}, u32[]{:S(2)}) %collective-permute-start.10) | collective-permute-done | bytes 65568 | tf_op jit(solution)/shard_map/ppermute | solution.py:339
  32.2 0.6 %write_dkv.1 = bf16[1,128,768]{2,1,0:T(8,128)(2,1)} custom-call(bf16[1,128,768]{2,1,0:T(8,128)(2,1)} %write_dq.1.filled_ref, bf16[128,256]{1,0:T(8,128)(2,1)S(1)} %collective-permute-done.10.dkv_ref), custom_call_target="tpu_custom_call", output_to_operand_aliasing={{}: (0, {})} | custom-call | tf_op jit(solution)/shard_map/write_dkv/pallas_call | solution.py:350
  (2 shorter events, 0.1 us)
Async XLA Ops:
  2.4 5.8 %collective-permute-start = (bf16[1032,128]{1,0:T(8,128)(2,1)S(1)}, bf16[1032,128]{1,0:T(8,128)(2,1)S(1)}, u32[]{:S(2)}, u32[]{:S(2)}) collective-permute-start(bf16[1032,128]{1,0:T(8,128)(2,1)S(1)} %fetch_qg.1.refs_0_.refs_5_), channel_id=1, source_target_pairs={{0,1},{1,0},{2,3},{3,2},{4,5},{5,4},{6,7},{7,6},{8,9},{9,8},{10,11... | collective-permute-start | bytes 792584 | tf_op jit(solution)/shard_map/ppermute | solution.py:32
  3.0 5.6 %collective-permute-start.3 = (bf16[264,128]{1,0:T(8,128)(2,1)S(1)}, bf16[264,128]{1,0:T(8,128)(2,1)S(1)}, u32[]{:S(2)}, u32[]{:S(2)}) collective-permute-start(bf16[264,128]{1,0:T(8,128)(2,1)S(1)} %fetch_kv.1.kv_ref.refs_2_.refs_7_.refs_5_), channel_id=1, source_target_pairs={{0,2},{1,3},{2,0},{3,1},{4,6},{5,7},{6,4},{7,5},{8,10},{9,11},{10,... | collective-permute-start | bytes 202760 | tf_op jit(solution)/shard_map/ppermute | solution.py:45
  5.6 6.9 %collective-permute-start.2 = (bf16[264,128]{1,0:T(8,128)(2,1)S(1)}, bf16[264,128]{1,0:T(8,128)(2,1)S(1)}, u32[]{:S(2)}, u32[]{:S(2)}) collective-permute-start(bf16[264,128]{1,0:T(8,128)(2,1)S(1)} %fetch_kv.1.kv_ref.refs_2_.refs_7_.refs_5_), channel_id=1, source_target_pairs={{0,6},{1,7},{2,4},{3,5},{4,2},{5,3},{6,0},{7,1},{8,14},{9,15},{10,... | collective-permute-start | bytes 202760 | tf_op jit(solution)/shard_map/ppermute | solution.py:45
  8.1 6.9 %collective-permute-start.1 = (bf16[264,128]{1,0:T(8,128)(2,1)S(1)}, bf16[264,128]{1,0:T(8,128)(2,1)S(1)}, u32[]{:S(2)}, u32[]{:S(2)}) collective-permute-start(bf16[264,128]{1,0:T(8,128)(2,1)S(1)} %fetch_kv.1.kv_ref.refs_2_.refs_7_.refs_5_), channel_id=1, source_target_pairs={{0,4},{1,5},{2,6},{3,7},{4,0},{5,1},{6,2},{7,3},{8,12},{9,13},{10,... | collective-permute-start | bytes 202760 | tf_op jit(solution)/shard_map/ppermute | solution.py:45
  15.4 1.3 %collective-permute-start.4 = (f32[8,1024]{1,0:T(8,128)S(1)}, f32[8,1024]{1,0:T(8,128)S(1)}, u32[]{:S(2)}, u32[]{:S(2)}) collective-permute-start(f32[8,1024]{1,0:T(8,128)S(1)} %get-tuple-element.31.refs_3_), channel_id=1, source_target_pairs={{0,1},{1,0},{2,3},{3,2},{4,5},{5,4},{6,7},{7,6},{8,9},{9,8},{10,11... | collective-permute-start | bytes 98312 | tf_op jit(solution)/shard_map/ppermute | solution.py:32
  18.1 5.2 %collective-permute-start.5 = (bf16[128,512]{1,0:T(8,128)(2,1)S(1)}, bf16[128,512]{1,0:T(8,128)(2,1)S(1)}, u32[]{:S(2)}, u32[]{:S(2)}) collective-permute-start(bf16[128,512]{1,0:T(8,128)(2,1)S(1)} %dq_other.1), channel_id=1, source_target_pairs={{0,1},{1,0},{2,3},{3,2},{4,5},{5,4},{6,7},{7,6},{8,9},{9,8},{10,11... | collective-permute-start | bytes 393224 | tf_op jit(solution)/shard_map/ppermute | solution.py:32
  18.4 7.5 %collective-permute-start.9 = (bf16[128,256]{1,0:T(8,128)(2,1)S(1)}, bf16[128,256]{1,0:T(8,128)(2,1)S(1)}, u32[]{:S(2)}, u32[]{:S(2)}) collective-permute-start(bf16[128,256]{1,0:T(8,128)(2,1)S(1)} %get-tuple-element.46), channel_id=1, source_target_pairs={{2,0},{3,1},{0,2},{1,3},{6,4},{7,5},{4,6},{5,7},{10,8},{11,9},{8,1... | collective-permute-start | bytes 196616 | tf_op jit(solution)/shard_map/ppermute | solution.py:49
  18.4 7.5 %collective-permute-start.8 = (bf16[128,256]{1,0:T(8,128)(2,1)S(1)}, bf16[128,256]{1,0:T(8,128)(2,1)S(1)}, u32[]{:S(2)}, u32[]{:S(2)}) collective-permute-start(bf16[128,256]{1,0:T(8,128)(2,1)S(1)} %get-tuple-element.45), channel_id=1, source_target_pairs={{4,0},{5,1},{6,2},{7,3},{0,4},{1,5},{2,6},{3,7},{12,8},{13,9},{14,... | collective-permute-start | bytes 196616 | tf_op jit(solution)/shard_map/ppermute | solution.py:49
  21.6 6.1 %collective-permute-start.7 = (bf16[128,256]{1,0:T(8,128)(2,1)S(1)}, bf16[128,256]{1,0:T(8,128)(2,1)S(1)}, u32[]{:S(2)}, u32[]{:S(2)}) collective-permute-start(bf16[128,256]{1,0:T(8,128)(2,1)S(1)} %get-tuple-element.44), channel_id=1, source_target_pairs={{6,0},{7,1},{4,2},{5,3},{2,4},{3,5},{0,6},{1,7},{14,8},{15,9},{12,... | collective-permute-start | bytes 196616 | tf_op jit(solution)/shard_map/ppermute | solution.py:49
  23.4 6.9 %collective-permute-start.6 = (bf16[128,512]{1,0:T(8,128)(2,1)S(1)}, bf16[128,512]{1,0:T(8,128)(2,1)S(1)}, u32[]{:S(2)}, u32[]{:S(2)}) collective-permute-start(bf16[128,512]{1,0:T(8,128)(2,1)S(1)} %add_convert_fusion), channel_id=1, source_target_pairs={{0,24},{8,0},{16,8},{24,16},{1,25},{9,1},{17,9},{25,17},{2,26},{10... | collective-permute-start | bytes 393224 | tf_op jit(solution)/shard_map/ppermute | solution.py:335
  27.7 4.4 %collective-permute-start.10 = (bf16[128,256]{1,0:T(8,128)(2,1)S(1)}, bf16[128,256]{1,0:T(8,128)(2,1)S(1)}, u32[]{:S(2)}, u32[]{:S(2)}) collective-permute-start(bf16[128,256]{1,0:T(8,128)(2,1)S(1)} %add_convert_fusion.1), channel_id=1, source_target_pairs={{0,24},{8,0},{16,8},{24,16},{1,25},{9,1},{17,9},{25,17},{2,26},{10... | collective-permute-start | bytes 196616 | tf_op jit(solution)/shard_map/ppermute | solution.py:339

commit v2 on v1

--- a/solution.py
+++ b/solution.py
@@ -219,8 +219,13 @@
         dq_ref[:, h * head : (h + 1) * head] = piece.astype(dq_ref.dtype)
 
 
-def far_grad_kernel(group, rows, head, *refs):
-    block_grads(group, rows, head, refs[0:5], refs[5:7], refs[7], refs[8])
+def far_grad_kernel(group, rows, head, span, *refs):
+    shared = refs[3 * span : 3 * span + 2]
+    qg_refs = refs[3 * span + 2 : 3 * span + 4]
+    outs = refs[3 * span + 4 :]
+    for i in range(span):
+        own = refs[3 * i : 3 * i + 3]
+        block_grads(group, rows, head, (*own, *shared), qg_refs, outs[2 * i], outs[2 * i + 1])
 
 
 def other_query_grad_kernel(blocks, group, rows, head, *refs):
@@ -298,15 +303,17 @@
     dkv_shape = jax.ShapeDtypeStruct((rows, 2 * head), jnp.bfloat16)
     half_square = jax.ShapeDtypeStruct((rows, 2 * width), jnp.bfloat16)
     returned, dscores = {}, {}
-    for j in steps:
-        dkv_part, dscores[j] = pl.pallas_call(
-            functools.partial(far_grad_kernel, group, rows, head),
-            out_shape=(dkv_shape, half_square),
-            in_specs=[vmem_spec()] * 7,
-            out_specs=(vmem_spec(),) * 2,
+    for part in grad_parts(count):
+        results = pl.pallas_call(
+            functools.partial(far_grad_kernel, group, rows, head, len(part)),
+            out_shape=(dkv_shape, half_square) * len(part),
+            in_specs=[vmem_spec()] * (3 * len(part) + 4),
+            out_specs=(vmem_spec(),) * (2 * len(part)),
             compiler_params=params(),
-        )(*scored[j][0:3], merged, merged_other, qg, qg_other)
-        returned[j] = chip_return(dkv_part, count, j)
+        )(*(x for j in part for x in scored[j][0:3]), merged, merged_other, qg, qg_other)
+        for i, j in enumerate(part):
+            dscores[j] = results[2 * i + 1]
+            returned[j] = chip_return(results[2 * i], count, j)
     near = (*scored[0][0:3], merged, merged_other)
     shared = (kv, *(kv_blocks[j] for j in steps), *(dscores[j] for j in steps))
     dq_other = pl.pallas_call(
@@ -368,6 +375,11 @@
     return [j for j in send_order(count) if j != half] + [half]
 
 
+def grad_parts(count):
+    steps = send_order(count)
+    return [steps[0:1], steps[1:]]
+
+
 def solution(mesh):
     in_specs = (
         P("section", None, "ctx", None),

time: 33.1 us -> 31.8 us (0.961)
  waiting for transfers between devices: 9.84 us -> 8.6 us
    ppermute x3, waiting for transfers between devices: 5.65 us -> 4.14 us  [chip_send(): return lax.ppermute(value, 'ctx', chip_pairs(count, step))]
    pallas_call x3 -> x2, Pallas kernels: 0.98 us -> 0.84 us  [per_device(): pl.pallas_call(functools.partial(far_grad_kernel, group, rows, head, len(...]
where the time goes in v2:
time: 31.8 us; the launch traced here: 31.5 us
  starting transfers between devices  15.7 us (49%)
  waiting for transfers between devices  8.6 us (27%)
  Pallas kernels  6.41 us (20%)
  between operations  0.76 us (2%)
    ppermute x3, starting transfers between devices, chip_send(): return lax.ppermute(value, 'ctx', chip_pairs(count, step))  5.31 us
    ppermute x3, starting transfers between devices, chip_return(): lax.ppermute(value, 'ctx', [(b, a) for a, b in chip_pairs(count, step)])  4.39 us
    ppermute x3, waiting for transfers between devices, chip_send(): return lax.ppermute(value, 'ctx', chip_pairs(count, step))  4.14 us
    ppermute x1, starting transfers between devices, per_device(): dq_message = lax.ppermute(dq, 'section', back)  2.61 us
    ppermute x1, starting transfers between devices, per_device(): dkv_message = lax.ppermute(dkv.astype(jnp.bfloat16), 'section', back)  2.5 us
    ppermute x3, waiting for transfers between devices, chip_return(): lax.ppermute(value, 'ctx', [(b, a) for a, b in chip_pairs(count, step)])  2.03 us
    pallas_call x4, Pallas kernels, per_device(): pl.pallas_call(functools.partial(score_kernel, group, rows, head, len(ear...  1.54 us
    ppermute x1, waiting for transfers between devices, per_device(): dkv_message = lax.ppermute(dkv.astype(jnp.bfloat16), 'section', back)  1.23 us
  transfers between devices with their start and end apart: 11, of which 5 were waited for; matrix products, arithmetic and copies ran while one was open for 0% of the time, Pallas kernels for 7%

profile of v2, /device:TPU:0, one launch (start us, length us, event | category | flops | bytes accessed | tf_op | source)
XLA Modules:
  0.0 31.5 jit_solution(9348824073669964169)
XLA Ops:
  0.7 0.8 %fetch_kv.1.kv_ref.refs_2_.refs_7_.refs_5_ = bf16[264,128]{1,0:T(8,128)(2,1)S(1)} custom-call(s32[1]{0:T(128)S(6)} %copy.9.slot_ref, s32[2]{0:T(128)} %ids_ref.1, bf16[1,8,128,128]{3,2,1,0:T(8,128)(2,1)} %key_ref.1, bf16[1,8,128,128]{3,2,1,0:T(8,128)(2,1)} %value_ref.1), custom_call_target="tpu_custom_call" | custom-call | tf_op jit(solution)/shard_map/fetch_kv/pallas_call | solution.py:261
  1.5 1.0 %fetch_qg.1.refs_0_.refs_5_.refs_8_ = bf16[1032,128]{1,0:T(8,128)(2,1)S(1)} custom-call(s32[1]{0:T(128)S(6)} %copy.9.slot_ref, bf16[1,8,128,512]{3,2,1,0:T(8,128)(2,1)} %query_ref.1, bf16[1,128,512]{2,1,0:T(8,128)(2,1)} %grad_ref.1, bf16[264,128]{1,0:T(8,128)(2,1)S(1)} %fetch_kv.1.kv_ref.refs_2_.refs_7_.refs_5_), custom_call_target="tpu_custom_call" | custom-call | tf_op jit(solution)/shard_map/fetch_qg/pallas_call | solution.py:270
  2.4 0.6 %collective-permute-start = (bf16[1032,128]{1,0:T(8,128)(2,1)S(1)}, bf16[1032,128]{1,0:T(8,128)(2,1)S(1)}, u32[]{:S(2)}, u32[]{:S(2)}) collective-permute-start(bf16[1032,128]{1,0:T(8,128)(2,1)S(1)} %fetch_qg.1.refs_0_.refs_5_.refs_8_), channel_id=1, source_target_pairs={{0,1},{1,0},{2,3},{3,2},{4,5},{5,4},{6,7},{7,6},{8,9},{9,8},{10,11... | collective-permute-start | bytes 792584 | tf_op jit(solution)/shard_map/ppermute | solution.py:32
  3.0 4.7 %collective-permute-start.2 = (bf16[264,128]{1,0:T(8,128)(2,1)S(1)}, bf16[264,128]{1,0:T(8,128)(2,1)S(1)}, u32[]{:S(2)}, u32[]{:S(2)}) collective-permute-start(bf16[264,128]{1,0:T(8,128)(2,1)S(1)} %fetch_kv.1.kv_ref.refs_2_.refs_7_.refs_5_), channel_id=1, source_target_pairs={{0,6},{1,7},{2,4},{3,5},{4,2},{5,3},{6,0},{7,1},{8,14},{9,15},{10,... | collective-permute-start | bytes 202760 | tf_op jit(solution)/shard_map/ppermute | solution.py:45
  7.6 0.0 collective-permute-start.3
  7.6 0.6 %collective-permute-start.1 = (bf16[264,128]{1,0:T(8,128)(2,1)S(1)}, bf16[264,128]{1,0:T(8,128)(2,1)S(1)}, u32[]{:S(2)}, u32[]{:S(2)}) collective-permute-start(bf16[264,128]{1,0:T(8,128)(2,1)S(1)} %fetch_kv.1.kv_ref.refs_2_.refs_7_.refs_5_), channel_id=1, source_target_pairs={{0,4},{1,5},{2,6},{3,7},{4,0},{5,1},{6,2},{7,3},{8,12},{9,13},{10,... | collective-permute-start | bytes 202760 | tf_op jit(solution)/shard_map/ppermute | solution.py:45
  8.3 0.0 collective-permute-done.refs_1_.refs_6_.refs_9_
  8.3 0.4 %shard_map.64 = (f32[128,1024]{1,0:T(8,128)S(1)}, f32[128,1024]{1,0:T(8,128)S(1)}, f32[8,1024]{1,0:T(8,128)S(1)}) custom-call(bf16[1032,128]{1,0:T(8,128)(2,1)S(1)} %fetch_qg.1.refs_0_.refs_5_.refs_8_, bf16[1032,128]{1,0:T(8,128)(2,1)S(1)} %collective-permute-done.refs_1_.refs_6_.refs_9_, bf16[264,128]{1,0:T(8,128)(2,1)S(1)} %fetch_kv.1.kv_ref.refs_2_.refs_7_.refs_5_), custom_call_target="tpu_custom_call" | custom-call | tf_op jit(solution)/shard_map/pallas_call | solution.py:293
  8.7 2.0 %collective-permute-done.2.refs_2_.refs_8_.refs_6_ = bf16[264,128]{1,0:T(8,128)(2,1)S(1)} collective-permute-done((bf16[264,128]{1,0:T(8,128)(2,1)S(1)}, bf16[264,128]{1,0:T(8,128)(2,1)S(1)}, u32[]{:S(2)}, u32[]{:S(2)}) %collective-permute-start.2) | collective-permute-done | bytes 67616 | tf_op jit(solution)/shard_map/ppermute | solution.py:45
  10.7 0.4 %shard_map.65 = (f32[128,1024]{1,0:T(8,128)S(1)}, f32[128,1024]{1,0:T(8,128)S(1)}, f32[8,1024]{1,0:T(8,128)S(1)}) custom-call(bf16[1032,128]{1,0:T(8,128)(2,1)S(1)} %fetch_qg.1.refs_0_.refs_5_.refs_8_, bf16[1032,128]{1,0:T(8,128)(2,1)S(1)} %collective-permute-done.refs_1_.refs_6_.refs_9_, bf16[264,128]{1,0:T(8,128)(2,1)S(1)} %collective-permute-done.2.refs_2_.refs_8_.refs_6_), custom_call_target="tpu_custom_call" | custom-call | tf_op jit(solution)/shard_map/pallas_call | solution.py:293
  11.1 2.1 %collective-permute-done.3.refs_2_.refs_10_.refs_8_ = bf16[264,128]{1,0:T(8,128)(2,1)S(1)} collective-permute-done((bf16[264,128]{1,0:T(8,128)(2,1)S(1)}, bf16[264,128]{1,0:T(8,128)(2,1)S(1)}, u32[]{:S(2)}, u32[]{:S(2)}) %collective-permute-start.3) | collective-permute-done | bytes 67616 | tf_op jit(solution)/shard_map/ppermute | solution.py:45
  13.2 0.4 %shard_map.66 = (f32[128,1024]{1,0:T(8,128)S(1)}, f32[128,1024]{1,0:T(8,128)S(1)}, f32[8,1024]{1,0:T(8,128)S(1)}) custom-call(bf16[1032,128]{1,0:T(8,128)(2,1)S(1)} %fetch_qg.1.refs_0_.refs_5_.refs_8_, bf16[1032,128]{1,0:T(8,128)(2,1)S(1)} %collective-permute-done.refs_1_.refs_6_.refs_9_, bf16[264,128]{1,0:T(8,128)(2,1)S(1)} %collective-permute-done.3.refs_2_.refs_10_.refs_8_), custom_call_target="tpu_custom_call" | custom-call | tf_op jit(solution)/shard_map/pallas_call | solution.py:293
  13.5 0.0 collective-permute-done.1.refs_2_.refs_9_.refs_7_
  13.6 0.4 %shard_map.67 = (f32[128,1024]{1,0:T(8,128)S(1)}, f32[128,1024]{1,0:T(8,128)S(1)}, f32[8,1024]{1,0:T(8,128)S(1)}, f32[8,1024]{1,0:T(8,128)S(1)}) custom-call(bf16[1032,128]{1,0:T(8,128)(2,1)S(1)} %fetch_qg.1.refs_0_.refs_5_.refs_8_, bf16[1032,128]{1,0:T(8,128)(2,1)S(1)} %collective-permute-done.refs_1_.refs_6_.refs_9_, ...), custom_call_target="tpu_custom_call" | custom-call | tf_op jit(solution)/shard_map/pallas_call | solution.py:293
  14.0 0.1 collective-permute-start.4
  14.1 1.2 %collective-permute-done.4.refs_4_.refs_7_ = f32[8,1024]{1,0:T(8,128)S(1)} collective-permute-done((f32[8,1024]{1,0:T(8,128)S(1)}, f32[8,1024]{1,0:T(8,128)S(1)}, u32[]{:S(2)}, u32[]{:S(2)}) %collective-permute-start.4) | collective-permute-done | bytes 32800 | tf_op jit(solution)/shard_map/ppermute | solution.py:32
  15.3 0.3 %shard_map.68 = (bf16[128,256]{1,0:T(8,128)(2,1)S(1)}, bf16[128,1024]{1,0:T(8,128)(2,1)S(1)}) custom-call(f32[128,1024]{1,0:T(8,128)S(1)} %get-tuple-element.32.refs_0_, f32[128,1024]{1,0:T(8,128)S(1)} %get-tuple-element.33.refs_1_, f32[8,1024]{1,0:T(8,128)S(1)} %get-tuple-element.29.refs_4_.refs_2_, f32[8,1024]{1,0:T(8,128)S(1)} %get-tuple-element.31.refs_3_.refs_6_, ...), custom_call_target="tpu_custom_call" | custom-call | tf_op jit(solution)/shard_map/pallas_call | solution.py:307
  15.6 0.5 %shard_map.69 = (bf16[128,256]{1,0:T(8,128)(2,1)S(1)}, bf16[128,1024]{1,0:T(8,128)(2,1)S(1)}, bf16[128,256]{1,0:T(8,128)(2,1)S(1)}, bf16[128,1024]{1,0:T(8,128)(2,1)S(1)}) custom-call(f32[128,1024]{1,0:T(8,128)S(1)} %get-tuple-element.35.refs_0_, f32[128,1024]{1,0:T(8,128)S(1)} %get-tuple-element.36.refs_1_, f32[8,1024]{1,0:T(8,128)S(1)} %get-tuple-element.37.refs_2_, ...), custom_call_target="tpu_custom_call" | custom-call | tf_op jit(solution)/shard_map/pallas_call | solution.py:307
  16.1 0.4 %dq_other.1 = bf16[128,512]{1,0:T(8,128)(2,1)S(1)} custom-call(f32[128,1024]{1,0:T(8,128)S(1)} %get-tuple-element.26.refs_0_, f32[128,1024]{1,0:T(8,128)S(1)} %get-tuple-element.27.refs_1_, f32[8,1024]{1,0:T(8,128)S(1)} %get-tuple-element.28.refs_3_.refs_2_, f32[8,1024]{1,0:T(8,128)S(1)} %get-tuple-element.31.refs_3_.refs_6_, ...), custom_call_target="tpu_custom_call" | custom-call | tf_op jit(solution)/shard_map/dq_other/pallas_call | solution.py:319
  16.6 0.2 collective-permute-start.5
  16.8 1.3 %collective-permute-start.9 = (bf16[128,256]{1,0:T(8,128)(2,1)S(1)}, bf16[128,256]{1,0:T(8,128)(2,1)S(1)}, u32[]{:S(2)}, u32[]{:S(2)}) collective-permute-start(bf16[128,256]{1,0:T(8,128)(2,1)S(1)} %get-tuple-element.46), channel_id=1, source_target_pairs={{2,0},{3,1},{0,2},{1,3},{6,4},{7,5},{4,6},{5,7},{10,8},{11,9},{8,1... | collective-permute-start | bytes 196616 | tf_op jit(solution)/shard_map/ppermute | solution.py:49
  18.1 1.6 %collective-permute-start.8 = (bf16[128,256]{1,0:T(8,128)(2,1)S(1)}, bf16[128,256]{1,0:T(8,128)(2,1)S(1)}, u32[]{:S(2)}, u32[]{:S(2)}) collective-permute-start(bf16[128,256]{1,0:T(8,128)(2,1)S(1)} %get-tuple-element.45), channel_id=1, source_target_pairs={{4,0},{5,1},{6,2},{7,3},{0,4},{1,5},{2,6},{3,7},{12,8},{13,9},{14,... | collective-permute-start | bytes 196616 | tf_op jit(solution)/shard_map/ppermute | solution.py:49
  19.7 1.5 %collective-permute-start.7 = (bf16[128,256]{1,0:T(8,128)(2,1)S(1)}, bf16[128,256]{1,0:T(8,128)(2,1)S(1)}, u32[]{:S(2)}, u32[]{:S(2)}) collective-permute-start(bf16[128,256]{1,0:T(8,128)(2,1)S(1)} %get-tuple-element.44), channel_id=1, source_target_pairs={{6,0},{7,1},{4,2},{5,3},{2,4},{3,5},{0,6},{1,7},{14,8},{15,9},{12,... | collective-permute-start | bytes 196616 | tf_op jit(solution)/shard_map/ppermute | solution.py:49
  21.2 0.5 %grads0.1 = (f32[128,256]{1,0:T(8,128)S(1)}, f32[128,512]{1,0:T(8,128)S(1)}) custom-call(f32[128,1024]{1,0:T(8,128)S(1)} %get-tuple-element.26.refs_0_, f32[128,1024]{1,0:T(8,128)S(1)} %get-tuple-element.27.refs_1_, f32[8,1024]{1,0:T(8,128)S(1)} %get-tuple-element.28.refs_3_.refs_2_, f32[8,1024]{1,0:T(8,128)S(1)} %get-tuple-element.31.refs_3_.refs_6_, ...), custom_call_target="tpu_custom_call" | custom-call | tf_op jit(solution)/shard_map/grads0/pallas_call | solution.py:328
  21.7 0.0 collective-permute-done.5
  21.8 2.6 %collective-permute-start.6 = (bf16[128,512]{1,0:T(8,128)(2,1)S(1)}, bf16[128,512]{1,0:T(8,128)(2,1)S(1)}, u32[]{:S(2)}, u32[]{:S(2)}) collective-permute-start(bf16[128,512]{1,0:T(8,128)(2,1)S(1)} %add_convert_fusion), channel_id=1, source_target_pairs={{0,24},{8,0},{16,8},{24,16},{1,25},{9,1},{17,9},{25,17},{2,26},{10... | collective-permute-start | bytes 393224 | tf_op jit(solution)/shard_map/ppermute | solution.py:342
  24.4 0.0 collective-permute-done.9
  24.4 2.0 %collective-permute-done.8 = bf16[128,256]{1,0:T(8,128)(2,1)S(1)} collective-permute-done((bf16[128,256]{1,0:T(8,128)(2,1)S(1)}, bf16[128,256]{1,0:T(8,128)(2,1)S(1)}, u32[]{:S(2)}, u32[]{:S(2)}) %collective-permute-start.8) | collective-permute-done | bytes 65568 | tf_op jit(solution)/shard_map/ppermute | solution.py:49
  26.4 0.0 collective-permute-done.7
  26.5 2.5 %collective-permute-start.10 = (bf16[128,256]{1,0:T(8,128)(2,1)S(1)}, bf16[128,256]{1,0:T(8,128)(2,1)S(1)}, u32[]{:S(2)}, u32[]{:S(2)}) collective-permute-start(bf16[128,256]{1,0:T(8,128)(2,1)S(1)} %add_convert_fusion.1), channel_id=1, source_target_pairs={{0,24},{8,0},{16,8},{24,16},{1,25},{9,1},{17,9},{25,17},{2,26},{10... | collective-permute-start | bytes 196616 | tf_op jit(solution)/shard_map/ppermute | solution.py:346
  29.0 0.0 collective-permute-done.6.dq_ref
  29.0 0.7 %write_dq.1.filled_ref = bf16[1,128,768]{2,1,0:T(8,128)(2,1)} custom-call(bf16[128,512]{1,0:T(8,128)(2,1)S(1)} %collective-permute-done.6.dq_ref), custom_call_target="tpu_custom_call" | custom-call | tf_op jit(solution)/shard_map/write_dq/pallas_call | solution.py:348
  29.6 1.2 %collective-permute-done.10.dkv_ref = bf16[128,256]{1,0:T(8,128)(2,1)S(1)} collective-permute-done((bf16[128,256]{1,0:T(8,128)(2,1)S(1)}, bf16[128,256]{1,0:T(8,128)(2,1)S(1)}, u32[]{:S(2)}, u32[]{:S(2)}) %collective-permute-start.10) | collective-permute-done | bytes 65568 | tf_op jit(solution)/shard_map/ppermute | solution.py:346
  30.9 0.6 %write_dkv.1 = bf16[1,128,768]{2,1,0:T(8,128)(2,1)} custom-call(bf16[1,128,768]{2,1,0:T(8,128)(2,1)} %write_dq.1.filled_ref, bf16[128,256]{1,0:T(8,128)(2,1)S(1)} %collective-permute-done.10.dkv_ref), custom_call_target="tpu_custom_call", output_to_operand_aliasing={{}: (0, {})} | custom-call | tf_op jit(solution)/shard_map/write_dkv/pallas_call | solution.py:357
  (2 shorter events, 0.1 us)
Async XLA Ops:
  2.4 5.9 %collective-permute-start = (bf16[1032,128]{1,0:T(8,128)(2,1)S(1)}, bf16[1032,128]{1,0:T(8,128)(2,1)S(1)}, u32[]{:S(2)}, u32[]{:S(2)}) collective-permute-start(bf16[1032,128]{1,0:T(8,128)(2,1)S(1)} %fetch_qg.1.refs_0_.refs_5_.refs_8_), channel_id=1, source_target_pairs={{0,1},{1,0},{2,3},{3,2},{4,5},{5,4},{6,7},{7,6},{8,9},{9,8},{10,11... | collective-permute-start | bytes 792584 | tf_op jit(solution)/shard_map/ppermute | solution.py:32
  3.0 7.7 %collective-permute-start.2 = (bf16[264,128]{1,0:T(8,128)(2,1)S(1)}, bf16[264,128]{1,0:T(8,128)(2,1)S(1)}, u32[]{:S(2)}, u32[]{:S(2)}) collective-permute-start(bf16[264,128]{1,0:T(8,128)(2,1)S(1)} %fetch_kv.1.kv_ref.refs_2_.refs_7_.refs_5_), channel_id=1, source_target_pairs={{0,6},{1,7},{2,4},{3,5},{4,2},{5,3},{6,0},{7,1},{8,14},{9,15},{10,... | collective-permute-start | bytes 202760 | tf_op jit(solution)/shard_map/ppermute | solution.py:45
  7.6 5.5 %collective-permute-start.3 = (bf16[264,128]{1,0:T(8,128)(2,1)S(1)}, bf16[264,128]{1,0:T(8,128)(2,1)S(1)}, u32[]{:S(2)}, u32[]{:S(2)}) collective-permute-start(bf16[264,128]{1,0:T(8,128)(2,1)S(1)} %fetch_kv.1.kv_ref.refs_2_.refs_7_.refs_5_), channel_id=1, source_target_pairs={{0,2},{1,3},{2,0},{3,1},{4,6},{5,7},{6,4},{7,5},{8,10},{9,11},{10,... | collective-permute-start | bytes 202760 | tf_op jit(solution)/shard_map/ppermute | solution.py:45
  7.6 5.9 %collective-permute-start.1 = (bf16[264,128]{1,0:T(8,128)(2,1)S(1)}, bf16[264,128]{1,0:T(8,128)(2,1)S(1)}, u32[]{:S(2)}, u32[]{:S(2)}) collective-permute-start(bf16[264,128]{1,0:T(8,128)(2,1)S(1)} %fetch_kv.1.kv_ref.refs_2_.refs_7_.refs_5_), channel_id=1, source_target_pairs={{0,4},{1,5},{2,6},{3,7},{4,0},{5,1},{6,2},{7,3},{8,12},{9,13},{10,... | collective-permute-start | bytes 202760 | tf_op jit(solution)/shard_map/ppermute | solution.py:45
  14.0 1.3 %collective-permute-start.4 = (f32[8,1024]{1,0:T(8,128)S(1)}, f32[8,1024]{1,0:T(8,128)S(1)}, u32[]{:S(2)}, u32[]{:S(2)}) collective-permute-start(f32[8,1024]{1,0:T(8,128)S(1)} %get-tuple-element.31.refs_3_.refs_6_), channel_id=1, source_target_pairs={{0,1},{1,0},{2,3},{3,2},{4,5},{5,4},{6,7},{7,6},{8,9},{9,8},{10,11... | collective-permute-start | bytes 98312 | tf_op jit(solution)/shard_map/ppermute | solution.py:32
  16.6 5.2 %collective-permute-start.5 = (bf16[128,512]{1,0:T(8,128)(2,1)S(1)}, bf16[128,512]{1,0:T(8,128)(2,1)S(1)}, u32[]{:S(2)}, u32[]{:S(2)}) collective-permute-start(bf16[128,512]{1,0:T(8,128)(2,1)S(1)} %dq_other.1), channel_id=1, source_target_pairs={{0,1},{1,0},{2,3},{3,2},{4,5},{5,4},{6,7},{7,6},{8,9},{9,8},{10,11... | collective-permute-start | bytes 393224 | tf_op jit(solution)/shard_map/ppermute | solution.py:32
  16.8 7.6 %collective-permute-start.9 = (bf16[128,256]{1,0:T(8,128)(2,1)S(1)}, bf16[128,256]{1,0:T(8,128)(2,1)S(1)}, u32[]{:S(2)}, u32[]{:S(2)}) collective-permute-start(bf16[128,256]{1,0:T(8,128)(2,1)S(1)} %get-tuple-element.46), channel_id=1, source_target_pairs={{2,0},{3,1},{0,2},{1,3},{6,4},{7,5},{4,6},{5,7},{10,8},{11,9},{8,1... | collective-permute-start | bytes 196616 | tf_op jit(solution)/shard_map/ppermute | solution.py:49
  18.1 8.3 %collective-permute-start.8 = (bf16[128,256]{1,0:T(8,128)(2,1)S(1)}, bf16[128,256]{1,0:T(8,128)(2,1)S(1)}, u32[]{:S(2)}, u32[]{:S(2)}) collective-permute-start(bf16[128,256]{1,0:T(8,128)(2,1)S(1)} %get-tuple-element.45), channel_id=1, source_target_pairs={{4,0},{5,1},{6,2},{7,3},{0,4},{1,5},{2,6},{3,7},{12,8},{13,9},{14,... | collective-permute-start | bytes 196616 | tf_op jit(solution)/shard_map/ppermute | solution.py:49
  19.7 6.7 %collective-permute-start.7 = (bf16[128,256]{1,0:T(8,128)(2,1)S(1)}, bf16[128,256]{1,0:T(8,128)(2,1)S(1)}, u32[]{:S(2)}, u32[]{:S(2)}) collective-permute-start(bf16[128,256]{1,0:T(8,128)(2,1)S(1)} %get-tuple-element.44), channel_id=1, source_target_pairs={{6,0},{7,1},{4,2},{5,3},{2,4},{3,5},{0,6},{1,7},{14,8},{15,9},{12,... | collective-permute-start | bytes 196616 | tf_op jit(solution)/shard_map/ppermute | solution.py:49
  21.8 7.2 %collective-permute-start.6 = (bf16[128,512]{1,0:T(8,128)(2,1)S(1)}, bf16[128,512]{1,0:T(8,128)(2,1)S(1)}, u32[]{:S(2)}, u32[]{:S(2)}) collective-permute-start(bf16[128,512]{1,0:T(8,128)(2,1)S(1)} %add_convert_fusion), channel_id=1, source_target_pairs={{0,24},{8,0},{16,8},{24,16},{1,25},{9,1},{17,9},{25,17},{2,26},{10... | collective-permute-start | bytes 393224 | tf_op jit(solution)/shard_map/ppermute | solution.py:342
  26.5 4.4 %collective-permute-start.10 = (bf16[128,256]{1,0:T(8,128)(2,1)S(1)}, bf16[128,256]{1,0:T(8,128)(2,1)S(1)}, u32[]{:S(2)}, u32[]{:S(2)}) collective-permute-start(bf16[128,256]{1,0:T(8,128)(2,1)S(1)} %add_convert_fusion.1), channel_id=1, source_target_pairs={{0,24},{8,0},{16,8},{24,16},{1,25},{9,1},{17,9},{25,17},{2,26},{10... | collective-permute-start | bytes 196616 | tf_op jit(solution)/shard_map/ppermute | solution.py:346

commit v3 on v2

--- a/solution.py
+++ b/solution.py
@@ -168,7 +168,7 @@
         stat_ref[3:8, lanes] = jnp.zeros((5, width), jnp.float32)
     if earlier:
         merged_ref = refs[6 + earlier]
-        parts = [ref[...] for ref in earlier_refs] + [stat_ref[...]]
+        parts = [ref[0:3, :] for ref in earlier_refs] + [stat_ref[0:3, :]]
         top = functools.reduce(jnp.maximum, [part[0:1] for part in parts])
         fades = [jnp.exp2(part[0:1] - top) for part in parts]
         merged_ref[0:1, :] = top
@@ -277,27 +277,33 @@
         name="fetch_qg",
     )(stash_slot, in_hbm(queries), in_hbm(out_grad), kv)
 
-    steps = send_order(count)
+    steps = return_order(count)
     arrivals = arrival_order(count)
     kv_blocks = {0: kv}
-    for j in steps:
+    for j in send_order(count):
         kv_blocks[j] = chip_send(kv, count, j)
     qg_other = partner_swap(qg, count)
 
     square = jax.ShapeDtypeStruct((rows, 2 * width), jnp.float32)
     lines = jax.ShapeDtypeStruct((8, 2 * width), jnp.float32)
-    scored = {}
+    scored, merged = {}, None
     for j in [0] + arrivals:
-        last = j == arrivals[-1]
-        earlier = [scored[i][2] for i in scored] if last else []
+        if j == arrivals[-1]:
+            earlier = [merged]
+        elif j == arrivals[-2]:
+            earlier = [scored[i][2] for i in scored]
+        else:
+            earlier = []
+        merging = 1 if earlier else 0
         scored[j] = pl.pallas_call(
             functools.partial(score_kernel, group, rows, head, len(earlier)),
-            out_shape=(square, square, lines) + ((lines,) if last else ()),
+            out_shape=(square, square, lines) + (lines,) * merging,
             in_specs=[vmem_spec()] * (3 + len(earlier)),
-            out_specs=(vmem_spec(),) * (4 if last else 3),
+            out_specs=(vmem_spec(),) * (3 + merging),
             compiler_params=params(),
         )(qg, qg_other, kv_blocks[j], *earlier)
-    merged = scored[arrivals[-1]][3]
+        if earlier:
+            merged = scored[j][3]
     merged_other = partner_swap(merged, count)
 
     dkv_shape = jax.ShapeDtypeStruct((rows, 2 * head), jnp.bfloat16)
@@ -367,16 +373,20 @@
 
 
 def send_order(count):
-    return list(reversed(range(1, count // 2)))
+    half = count // 4
+    return [j for j in reversed(range(1, count // 2)) if j != half] + [half]
+
+
+def return_order(count):
+    return send_order(count)
 
 
 def arrival_order(count):
-    half = count // 4
-    return [j for j in send_order(count) if j != half] + [half]
+    return send_order(count)
 
 
 def grad_parts(count):
-    steps = send_order(count)
+    steps = return_order(count)
     return [steps[0:1], steps[1:]]
 
 

time: 31.8 us -> 31.1 us (0.978)
  waiting for transfers between devices: 8.6 us -> 7.89 us
    ppermute x3, waiting for transfers between devices: 2.03 us -> 1.33 us  [chip_return(): lax.ppermute(value, 'ctx', [(b, a) for a, b in chip_pairs(count, step)])]
  transfers between devices with their start and end apart: 11 -> 11, of which waited for: 5 -> 5; matrix products, arithmetic and copies ran while one was open for 0% -> 0% of each run, Pallas kernels for 7% -> 8%
where the time goes in v3:
time: 31.1 us; the launch traced here: 30.8 us
  starting transfers between devices  15.7 us (50%)
  waiting for transfers between devices  7.89 us (25%)
  Pallas kernels  6.44 us (21%)
  between operations  0.77 us (2%)
    ppermute x3, starting transfers between devices, chip_send(): return lax.ppermute(value, 'ctx', chip_pairs(count, step))  5.31 us
    ppermute x3, starting transfers between devices, chip_return(): lax.ppermute(value, 'ctx', [(b, a) for a, b in chip_pairs(count, step)])  4.39 us
    ppermute x3, waiting for transfers between devices, chip_send(): return lax.ppermute(value, 'ctx', chip_pairs(count, step))  4.13 us
    ppermute x1, starting transfers between devices, per_device(): dq_message = lax.ppermute(dq, 'section', back)  2.61 us
    ppermute x1, starting transfers between devices, per_device(): dkv_message = lax.ppermute(dkv.astype(jnp.bfloat16), 'section', back)  2.5 us
    pallas_call x4, Pallas kernels, per_device(): pl.pallas_call(functools.partial(score_kernel, group, rows, head, len(ear...  1.57 us
    ppermute x3, waiting for transfers between devices, chip_return(): lax.ppermute(value, 'ctx', [(b, a) for a, b in chip_pairs(count, step)])  1.33 us
    ppermute x1, waiting for transfers between devices, per_device(): dkv_message = lax.ppermute(dkv.astype(jnp.bfloat16), 'section', back)  1.23 us
  transfers between devices with their start and end apart: 11, of which 5 were waited for; matrix products, arithmetic and copies ran while one was open for 0% of the time, Pallas kernels for 8%

profile of v3, /device:TPU:0, one launch (start us, length us, event | category | flops | bytes accessed | tf_op | source)
XLA Modules:
  0.0 30.8 jit_solution(7918918813802121530)
XLA Ops:
  0.7 0.8 %fetch_kv.1.kv_ref.refs_2_.refs_7_.refs_5_ = bf16[264,128]{1,0:T(8,128)(2,1)S(1)} custom-call(s32[1]{0:T(128)S(6)} %copy.9.slot_ref, s32[2]{0:T(128)} %ids_ref.1, bf16[1,8,128,128]{3,2,1,0:T(8,128)(2,1)} %key_ref.1, bf16[1,8,128,128]{3,2,1,0:T(8,128)(2,1)} %value_ref.1), custom_call_target="tpu_custom_call" | custom-call | tf_op jit(solution)/shard_map/fetch_kv/pallas_call | solution.py:261
  1.5 1.0 %fetch_qg.1.refs_0_.refs_5_.refs_8_ = bf16[1032,128]{1,0:T(8,128)(2,1)S(1)} custom-call(s32[1]{0:T(128)S(6)} %copy.9.slot_ref, bf16[1,8,128,512]{3,2,1,0:T(8,128)(2,1)} %query_ref.1, bf16[1,128,512]{2,1,0:T(8,128)(2,1)} %grad_ref.1, bf16[264,128]{1,0:T(8,128)(2,1)S(1)} %fetch_kv.1.kv_ref.refs_2_.refs_7_.refs_5_), custom_call_target="tpu_custom_call" | custom-call | tf_op jit(solution)/shard_map/fetch_qg/pallas_call | solution.py:270
  2.4 0.6 %collective-permute-start = (bf16[1032,128]{1,0:T(8,128)(2,1)S(1)}, bf16[1032,128]{1,0:T(8,128)(2,1)S(1)}, u32[]{:S(2)}, u32[]{:S(2)}) collective-permute-start(bf16[1032,128]{1,0:T(8,128)(2,1)S(1)} %fetch_qg.1.refs_0_.refs_5_.refs_8_), channel_id=1, source_target_pairs={{0,1},{1,0},{2,3},{3,2},{4,5},{5,4},{6,7},{7,6},{8,9},{9,8},{10,11... | collective-permute-start | bytes 792584 | tf_op jit(solution)/shard_map/ppermute | solution.py:32
  3.0 4.7 %collective-permute-start.3 = (bf16[264,128]{1,0:T(8,128)(2,1)S(1)}, bf16[264,128]{1,0:T(8,128)(2,1)S(1)}, u32[]{:S(2)}, u32[]{:S(2)}) collective-permute-start(bf16[264,128]{1,0:T(8,128)(2,1)S(1)} %fetch_kv.1.kv_ref.refs_2_.refs_7_.refs_5_), channel_id=1, source_target_pairs={{0,6},{1,7},{2,4},{3,5},{4,2},{5,3},{6,0},{7,1},{8,14},{9,15},{10,... | collective-permute-start | bytes 202760 | tf_op jit(solution)/shard_map/ppermute | solution.py:45
  7.6 0.0 collective-permute-start.2
  7.6 0.6 %collective-permute-start.1 = (bf16[264,128]{1,0:T(8,128)(2,1)S(1)}, bf16[264,128]{1,0:T(8,128)(2,1)S(1)}, u32[]{:S(2)}, u32[]{:S(2)}) collective-permute-start(bf16[264,128]{1,0:T(8,128)(2,1)S(1)} %fetch_kv.1.kv_ref.refs_2_.refs_7_.refs_5_), channel_id=1, source_target_pairs={{0,4},{1,5},{2,6},{3,7},{4,0},{5,1},{6,2},{7,3},{8,12},{9,13},{10,... | collective-permute-start | bytes 202760 | tf_op jit(solution)/shard_map/ppermute | solution.py:45
  8.3 0.0 collective-permute-done.refs_1_.refs_6_.refs_9_
  8.3 0.4 %shard_map.64 = (f32[128,1024]{1,0:T(8,128)S(1)}, f32[128,1024]{1,0:T(8,128)S(1)}, f32[8,1024]{1,0:T(8,128)S(1)}) custom-call(bf16[1032,128]{1,0:T(8,128)(2,1)S(1)} %fetch_qg.1.refs_0_.refs_5_.refs_8_, bf16[1032,128]{1,0:T(8,128)(2,1)S(1)} %collective-permute-done.refs_1_.refs_6_.refs_9_, bf16[264,128]{1,0:T(8,128)(2,1)S(1)} %fetch_kv.1.kv_ref.refs_2_.refs_7_.refs_5_), custom_call_target="tpu_custom_call" | custom-call | tf_op jit(solution)/shard_map/pallas_call | solution.py:298
  8.7 2.0 %collective-permute-done.3.refs_2_.refs_8_.refs_6_ = bf16[264,128]{1,0:T(8,128)(2,1)S(1)} collective-permute-done((bf16[264,128]{1,0:T(8,128)(2,1)S(1)}, bf16[264,128]{1,0:T(8,128)(2,1)S(1)}, u32[]{:S(2)}, u32[]{:S(2)}) %collective-permute-start.3) | collective-permute-done | bytes 67616 | tf_op jit(solution)/shard_map/ppermute | solution.py:45
  10.7 0.4 %shard_map.65 = (f32[128,1024]{1,0:T(8,128)S(1)}, f32[128,1024]{1,0:T(8,128)S(1)}, f32[8,1024]{1,0:T(8,128)S(1)}) custom-call(bf16[1032,128]{1,0:T(8,128)(2,1)S(1)} %fetch_qg.1.refs_0_.refs_5_.refs_8_, bf16[1032,128]{1,0:T(8,128)(2,1)S(1)} %collective-permute-done.refs_1_.refs_6_.refs_9_, bf16[264,128]{1,0:T(8,128)(2,1)S(1)} %collective-permute-done.3.refs_2_.refs_8_.refs_6_), custom_call_target="tpu_custom_call" | custom-call | tf_op jit(solution)/shard_map/pallas_call | solution.py:298
  11.1 2.1 %collective-permute-done.2.refs_2_.refs_9_.refs_7_ = bf16[264,128]{1,0:T(8,128)(2,1)S(1)} collective-permute-done((bf16[264,128]{1,0:T(8,128)(2,1)S(1)}, bf16[264,128]{1,0:T(8,128)(2,1)S(1)}, u32[]{:S(2)}, u32[]{:S(2)}) %collective-permute-start.2) | collective-permute-done | bytes 67616 | tf_op jit(solution)/shard_map/ppermute | solution.py:45
  13.2 0.4 %shard_map.66 = (f32[128,1024]{1,0:T(8,128)S(1)}, f32[128,1024]{1,0:T(8,128)S(1)}, f32[8,1024]{1,0:T(8,128)S(1)}, f32[8,1024]{1,0:T(8,128)S(1)}) custom-call(bf16[1032,128]{1,0:T(8,128)(2,1)S(1)} %fetch_qg.1.refs_0_.refs_5_.refs_8_, bf16[1032,128]{1,0:T(8,128)(2,1)S(1)} %collective-permute-done.refs_1_.refs_6_.refs_9_, ...), custom_call_target="tpu_custom_call" | custom-call | tf_op jit(solution)/shard_map/pallas_call | solution.py:298
  13.6 0.0 collective-permute-done.1.refs_2_.refs_10_.refs_8_
  13.6 0.4 %shard_map.67 = (f32[128,1024]{1,0:T(8,128)S(1)}, f32[128,1024]{1,0:T(8,128)S(1)}, f32[8,1024]{1,0:T(8,128)S(1)}, f32[8,1024]{1,0:T(8,128)S(1)}) custom-call(bf16[1032,128]{1,0:T(8,128)(2,1)S(1)} %fetch_qg.1.refs_0_.refs_5_.refs_8_, bf16[1032,128]{1,0:T(8,128)(2,1)S(1)} %collective-permute-done.refs_1_.refs_6_.refs_9_, ...), custom_call_target="tpu_custom_call" | custom-call | tf_op jit(solution)/shard_map/pallas_call | solution.py:298
  14.0 0.1 collective-permute-start.4
  14.1 1.2 %collective-permute-done.4.refs_4_.refs_7_ = f32[8,1024]{1,0:T(8,128)S(1)} collective-permute-done((f32[8,1024]{1,0:T(8,128)S(1)}, f32[8,1024]{1,0:T(8,128)S(1)}, u32[]{:S(2)}, u32[]{:S(2)}) %collective-permute-start.4) | collective-permute-done | bytes 32800 | tf_op jit(solution)/shard_map/ppermute | solution.py:32
  15.3 0.3 %shard_map.68 = (bf16[128,256]{1,0:T(8,128)(2,1)S(1)}, bf16[128,1024]{1,0:T(8,128)(2,1)S(1)}) custom-call(f32[128,1024]{1,0:T(8,128)S(1)} %get-tuple-element.33.refs_0_, f32[128,1024]{1,0:T(8,128)S(1)} %get-tuple-element.34.refs_1_, f32[8,1024]{1,0:T(8,128)S(1)} %get-tuple-element.30.refs_4_.refs_2_, f32[8,1024]{1,0:T(8,128)S(1)} %get-tuple-element.32.refs_3_.refs_6_, ...), custom_call_target="tpu_custom_call" | custom-call | tf_op jit(solution)/shard_map/pallas_call | solution.py:313
  15.6 0.5 %shard_map.69 = (bf16[128,256]{1,0:T(8,128)(2,1)S(1)}, bf16[128,1024]{1,0:T(8,128)(2,1)S(1)}, bf16[128,256]{1,0:T(8,128)(2,1)S(1)}, bf16[128,1024]{1,0:T(8,128)(2,1)S(1)}) custom-call(f32[128,1024]{1,0:T(8,128)S(1)} %get-tuple-element.36.refs_0_, f32[128,1024]{1,0:T(8,128)S(1)} %get-tuple-element.37.refs_1_, f32[8,1024]{1,0:T(8,128)S(1)} %get-tuple-element.38.refs_2_, ...), custom_call_target="tpu_custom_call" | custom-call | tf_op jit(solution)/shard_map/pallas_call | solution.py:313
  16.1 0.4 %dq_other.1 = bf16[128,512]{1,0:T(8,128)(2,1)S(1)} custom-call(f32[128,1024]{1,0:T(8,128)S(1)} %get-tuple-element.27.refs_0_, f32[128,1024]{1,0:T(8,128)S(1)} %get-tuple-element.28.refs_1_, f32[8,1024]{1,0:T(8,128)S(1)} %get-tuple-element.29.refs_3_.refs_2_, f32[8,1024]{1,0:T(8,128)S(1)} %get-tuple-element.32.refs_3_.refs_6_, ...), custom_call_target="tpu_custom_call" | custom-call | tf_op jit(solution)/shard_map/dq_other/pallas_call | solution.py:325
  16.6 0.2 collective-permute-start.5
  16.8 2.3 %collective-permute-start.9 = (bf16[128,256]{1,0:T(8,128)(2,1)S(1)}, bf16[128,256]{1,0:T(8,128)(2,1)S(1)}, u32[]{:S(2)}, u32[]{:S(2)}) collective-permute-start(bf16[128,256]{1,0:T(8,128)(2,1)S(1)} %get-tuple-element.48), channel_id=1, source_target_pairs={{4,0},{5,1},{6,2},{7,3},{0,4},{1,5},{2,6},{3,7},{12,8},{13,9},{14,... | collective-permute-start | bytes 196616 | tf_op jit(solution)/shard_map/ppermute | solution.py:49
  19.1 0.6 %collective-permute-start.8 = (bf16[128,256]{1,0:T(8,128)(2,1)S(1)}, bf16[128,256]{1,0:T(8,128)(2,1)S(1)}, u32[]{:S(2)}, u32[]{:S(2)}) collective-permute-start(bf16[128,256]{1,0:T(8,128)(2,1)S(1)} %get-tuple-element.47), channel_id=1, source_target_pairs={{2,0},{3,1},{0,2},{1,3},{6,4},{7,5},{4,6},{5,7},{10,8},{11,9},{8,1... | collective-permute-start | bytes 196616 | tf_op jit(solution)/shard_map/ppermute | solution.py:49
  19.7 1.5 %collective-permute-start.7 = (bf16[128,256]{1,0:T(8,128)(2,1)S(1)}, bf16[128,256]{1,0:T(8,128)(2,1)S(1)}, u32[]{:S(2)}, u32[]{:S(2)}) collective-permute-start(bf16[128,256]{1,0:T(8,128)(2,1)S(1)} %get-tuple-element.46), channel_id=1, source_target_pairs={{6,0},{7,1},{4,2},{5,3},{2,4},{3,5},{0,6},{1,7},{14,8},{15,9},{12,... | collective-permute-start | bytes 196616 | tf_op jit(solution)/shard_map/ppermute | solution.py:49
  21.2 0.5 %grads0.1 = (f32[128,256]{1,0:T(8,128)S(1)}, f32[128,512]{1,0:T(8,128)S(1)}) custom-call(f32[128,1024]{1,0:T(8,128)S(1)} %get-tuple-element.27.refs_0_, f32[128,1024]{1,0:T(8,128)S(1)} %get-tuple-element.28.refs_1_, f32[8,1024]{1,0:T(8,128)S(1)} %get-tuple-element.29.refs_3_.refs_2_, f32[8,1024]{1,0:T(8,128)S(1)} %get-tuple-element.32.refs_3_.refs_6_, ...), custom_call_target="tpu_custom_call" | custom-call | tf_op jit(solution)/shard_map/grads0/pallas_call | solution.py:334
  21.8 0.0 collective-permute-done.5
  21.8 2.6 %collective-permute-start.6 = (bf16[128,512]{1,0:T(8,128)(2,1)S(1)}, bf16[128,512]{1,0:T(8,128)(2,1)S(1)}, u32[]{:S(2)}, u32[]{:S(2)}) collective-permute-start(bf16[128,512]{1,0:T(8,128)(2,1)S(1)} %add_convert_fusion), channel_id=1, source_target_pairs={{0,24},{8,0},{16,8},{24,16},{1,25},{9,1},{17,9},{25,17},{2,26},{10... | collective-permute-start | bytes 393224 | tf_op jit(solution)/shard_map/ppermute | solution.py:348
  24.4 0.0 collective-permute-done.9
  24.4 0.0 collective-permute-done.8
  24.4 1.3 %collective-permute-done.7 = bf16[128,256]{1,0:T(8,128)(2,1)S(1)} collective-permute-done((bf16[128,256]{1,0:T(8,128)(2,1)S(1)}, bf16[128,256]{1,0:T(8,128)(2,1)S(1)}, u32[]{:S(2)}, u32[]{:S(2)}) %collective-permute-start.7) | collective-permute-done | bytes 65568 | tf_op jit(solution)/shard_map/ppermute | solution.py:49
  25.8 2.5 %collective-permute-start.10 = (bf16[128,256]{1,0:T(8,128)(2,1)S(1)}, bf16[128,256]{1,0:T(8,128)(2,1)S(1)}, u32[]{:S(2)}, u32[]{:S(2)}) collective-permute-start(bf16[128,256]{1,0:T(8,128)(2,1)S(1)} %add_convert_fusion.1), channel_id=1, source_target_pairs={{0,24},{8,0},{16,8},{24,16},{1,25},{9,1},{17,9},{25,17},{2,26},{10... | collective-permute-start | bytes 196616 | tf_op jit(solution)/shard_map/ppermute | solution.py:352
  28.3 0.0 collective-permute-done.6.dq_ref
  28.3 0.7 %write_dq.1.filled_ref = bf16[1,128,768]{2,1,0:T(8,128)(2,1)} custom-call(bf16[128,512]{1,0:T(8,128)(2,1)S(1)} %collective-permute-done.6.dq_ref), custom_call_target="tpu_custom_call" | custom-call | tf_op jit(solution)/shard_map/write_dq/pallas_call | solution.py:354
  29.0 1.2 %collective-permute-done.10.dkv_ref = bf16[128,256]{1,0:T(8,128)(2,1)S(1)} collective-permute-done((bf16[128,256]{1,0:T(8,128)(2,1)S(1)}, bf16[128,256]{1,0:T(8,128)(2,1)S(1)}, u32[]{:S(2)}, u32[]{:S(2)}) %collective-permute-start.10) | collective-permute-done | bytes 65568 | tf_op jit(solution)/shard_map/ppermute | solution.py:352
  30.2 0.6 %write_dkv.1 = bf16[1,128,768]{2,1,0:T(8,128)(2,1)} custom-call(bf16[1,128,768]{2,1,0:T(8,128)(2,1)} %write_dq.1.filled_ref, bf16[128,256]{1,0:T(8,128)(2,1)S(1)} %collective-permute-done.10.dkv_ref), custom_call_target="tpu_custom_call", output_to_operand_aliasing={{}: (0, {})} | custom-call | tf_op jit(solution)/shard_map/write_dkv/pallas_call | solution.py:363
  (2 shorter events, 0.1 us)
Async XLA Ops:
  2.4 5.9 %collective-permute-start = (bf16[1032,128]{1,0:T(8,128)(2,1)S(1)}, bf16[1032,128]{1,0:T(8,128)(2,1)S(1)}, u32[]{:S(2)}, u32[]{:S(2)}) collective-permute-start(bf16[1032,128]{1,0:T(8,128)(2,1)S(1)} %fetch_qg.1.refs_0_.refs_5_.refs_8_), channel_id=1, source_target_pairs={{0,1},{1,0},{2,3},{3,2},{4,5},{5,4},{6,7},{7,6},{8,9},{9,8},{10,11... | collective-permute-start | bytes 792584 | tf_op jit(solution)/shard_map/ppermute | solution.py:32
  3.0 7.7 %collective-permute-start.3 = (bf16[264,128]{1,0:T(8,128)(2,1)S(1)}, bf16[264,128]{1,0:T(8,128)(2,1)S(1)}, u32[]{:S(2)}, u32[]{:S(2)}) collective-permute-start(bf16[264,128]{1,0:T(8,128)(2,1)S(1)} %fetch_kv.1.kv_ref.refs_2_.refs_7_.refs_5_), channel_id=1, source_target_pairs={{0,6},{1,7},{2,4},{3,5},{4,2},{5,3},{6,0},{7,1},{8,14},{9,15},{10,... | collective-permute-start | bytes 202760 | tf_op jit(solution)/shard_map/ppermute | solution.py:45
  7.6 5.5 %collective-permute-start.2 = (bf16[264,128]{1,0:T(8,128)(2,1)S(1)}, bf16[264,128]{1,0:T(8,128)(2,1)S(1)}, u32[]{:S(2)}, u32[]{:S(2)}) collective-permute-start(bf16[264,128]{1,0:T(8,128)(2,1)S(1)} %fetch_kv.1.kv_ref.refs_2_.refs_7_.refs_5_), channel_id=1, source_target_pairs={{0,2},{1,3},{2,0},{3,1},{4,6},{5,7},{6,4},{7,5},{8,10},{9,11},{10,... | collective-permute-start | bytes 202760 | tf_op jit(solution)/shard_map/ppermute | solution.py:45
  7.6 6.0 %collective-permute-start.1 = (bf16[264,128]{1,0:T(8,128)(2,1)S(1)}, bf16[264,128]{1,0:T(8,128)(2,1)S(1)}, u32[]{:S(2)}, u32[]{:S(2)}) collective-permute-start(bf16[264,128]{1,0:T(8,128)(2,1)S(1)} %fetch_kv.1.kv_ref.refs_2_.refs_7_.refs_5_), channel_id=1, source_target_pairs={{0,4},{1,5},{2,6},{3,7},{4,0},{5,1},{6,2},{7,3},{8,12},{9,13},{10,... | collective-permute-start | bytes 202760 | tf_op jit(solution)/shard_map/ppermute | solution.py:45
  14.0 1.3 %collective-permute-start.4 = (f32[8,1024]{1,0:T(8,128)S(1)}, f32[8,1024]{1,0:T(8,128)S(1)}, u32[]{:S(2)}, u32[]{:S(2)}) collective-permute-start(f32[8,1024]{1,0:T(8,128)S(1)} %get-tuple-element.32.refs_3_.refs_6_), channel_id=1, source_target_pairs={{0,1},{1,0},{2,3},{3,2},{4,5},{5,4},{6,7},{7,6},{8,9},{9,8},{10,11... | collective-permute-start | bytes 98312 | tf_op jit(solution)/shard_map/ppermute | solution.py:32
  16.6 5.2 %collective-permute-start.5 = (bf16[128,512]{1,0:T(8,128)(2,1)S(1)}, bf16[128,512]{1,0:T(8,128)(2,1)S(1)}, u32[]{:S(2)}, u32[]{:S(2)}) collective-permute-start(bf16[128,512]{1,0:T(8,128)(2,1)S(1)} %dq_other.1), channel_id=1, source_target_pairs={{0,1},{1,0},{2,3},{3,2},{4,5},{5,4},{6,7},{7,6},{8,9},{9,8},{10,11... | collective-permute-start | bytes 393224 | tf_op jit(solution)/shard_map/ppermute | solution.py:32
  16.8 7.6 %collective-permute-start.9 = (bf16[128,256]{1,0:T(8,128)(2,1)S(1)}, bf16[128,256]{1,0:T(8,128)(2,1)S(1)}, u32[]{:S(2)}, u32[]{:S(2)}) collective-permute-start(bf16[128,256]{1,0:T(8,128)(2,1)S(1)} %get-tuple-element.48), channel_id=1, source_target_pairs={{4,0},{5,1},{6,2},{7,3},{0,4},{1,5},{2,6},{3,7},{12,8},{13,9},{14,... | collective-permute-start | bytes 196616 | tf_op jit(solution)/shard_map/ppermute | solution.py:49
  19.1 5.3 %collective-permute-start.8 = (bf16[128,256]{1,0:T(8,128)(2,1)S(1)}, bf16[128,256]{1,0:T(8,128)(2,1)S(1)}, u32[]{:S(2)}, u32[]{:S(2)}) collective-permute-start(bf16[128,256]{1,0:T(8,128)(2,1)S(1)} %get-tuple-element.47), channel_id=1, source_target_pairs={{2,0},{3,1},{0,2},{1,3},{6,4},{7,5},{4,6},{5,7},{10,8},{11,9},{8,1... | collective-permute-start | bytes 196616 | tf_op jit(solution)/shard_map/ppermute | solution.py:49
  19.7 6.1 %collective-permute-start.7 = (bf16[128,256]{1,0:T(8,128)(2,1)S(1)}, bf16[128,256]{1,0:T(8,128)(2,1)S(1)}, u32[]{:S(2)}, u32[]{:S(2)}) collective-permute-start(bf16[128,256]{1,0:T(8,128)(2,1)S(1)} %get-tuple-element.46), channel_id=1, source_target_pairs={{6,0},{7,1},{4,2},{5,3},{2,4},{3,5},{0,6},{1,7},{14,8},{15,9},{12,... | collective-permute-start | bytes 196616 | tf_op jit(solution)/shard_map/ppermute | solution.py:49
  21.8 6.5 %collective-permute-start.6 = (bf16[128,512]{1,0:T(8,128)(2,1)S(1)}, bf16[128,512]{1,0:T(8,128)(2,1)S(1)}, u32[]{:S(2)}, u32[]{:S(2)}) collective-permute-start(bf16[128,512]{1,0:T(8,128)(2,1)S(1)} %add_convert_fusion), channel_id=1, source_target_pairs={{0,24},{8,0},{16,8},{24,16},{1,25},{9,1},{17,9},{25,17},{2,26},{10... | collective-permute-start | bytes 393224 | tf_op jit(solution)/shard_map/ppermute | solution.py:348
  25.8 4.4 %collective-permute-start.10 = (bf16[128,256]{1,0:T(8,128)(2,1)S(1)}, bf16[128,256]{1,0:T(8,128)(2,1)S(1)}, u32[]{:S(2)}, u32[]{:S(2)}) collective-permute-start(bf16[128,256]{1,0:T(8,128)(2,1)S(1)} %add_convert_fusion.1), channel_id=1, source_target_pairs={{0,24},{8,0},{16,8},{24,16},{1,25},{9,1},{17,9},{25,17},{2,26},{10... | collective-permute-start | bytes 196616 | tf_op jit(solution)/shard_map/ppermute | solution.py:352
